TPU v7x, 32 devices: a whole 2x2x4 slice. The times are simulated.
32 devices in a mesh: patch: 32 (over z, y, x, core).
Axes of the slice: x: 2, y: 2, z: 4, core: 2. Of those that a mesh axis runs over, the one named last changes fastest.
Arguments:
- grid_latent: bfloat16 [131072, 512], P('patch'), may hold values from -6 to 6
- mesh_latent: bfloat16 [10240, 512], P('patch'), may hold values from -6 to 6
- mesh_cotangent: bfloat16 [10240, 512], P('patch'), may hold values from -6 to 6
- grid_rows: int32 [12288], P('patch'), may hold values from 0 to 4095
- mesh_rows: int32 [12288], P('patch'), may hold values from 0 to 319
- counts: int32 [32, 32], P('patch'), may hold values from 1 to 12, as said below
- w1_grid: bfloat16 [512, 512], replicated, may hold values from -0.25 to 0.25
- w1_mesh: bfloat16 [512, 512], replicated, may hold values from -0.25 to 0.25
- bias_one: float32 [512], replicated, may hold values from -3 to 3
- w2: bfloat16 [512, 512], replicated, may hold values from -0.25 to 0.25
Outputs:
- grid_grad: float32 [131072, 512], P('patch')
- mesh_grad: float32 [10240, 512], P('patch')
- w1_grid_grad: float32 [512, 512], replicated
- w1_mesh_grad: float32 [512, 512], replicated
- w2_grad: float32 [512, 512], replicated
- bias_grad: float32 [512], replicated
Inputs may be any that keep to these rules, and one draw needn't show every extreme that they name: counts[p, q] of the 12 slots from patch p to owner q are live, the first ones; every row and every column of counts has at least one entry equal to 12. `grid_rows`: padding slots hold arbitrary rows in range.
All inputs are finite; a program needn't handle non-finite values.
Results may differ from a plain program's by a relative error of at most 0.007.
Values may be sent and summed in bfloat16 or wider, within the bound.
No kernel may reach another device: no remote copies, remote signals or barrier semaphores. Data moves between devices by JAX's collectives and lax.ppermute only.
A program may use at most 128 MiB of HBM per device.

v0:
```python
import math

import jax
import jax.numpy as jnp
from jax import lax
from jax.sharding import PartitionSpec as P


def swish_parts(before):
    logistic = jax.nn.sigmoid(before)
    return (before * logistic, logistic * (1.0 + before * (1.0 - logistic)))


def body(
    grid_latent,
    mesh_latent,
    mesh_cotangent,
    grid_rows,
    mesh_rows,
    counts,
    w1_grid,
    w1_mesh,
    bias_one,
    w2,
):
    members = lax.axis_size("patch")
    slot_count = grid_rows.shape[0]
    capacity = slot_count // members
    live_mask = (jnp.arange(capacity, dtype=jnp.int32)[None, :] < counts[0][:, None]).reshape(
        slot_count
    )
    wanted = lax.all_to_all(grid_rows, "patch", split_axis=0, concat_axis=0, tiled=True)
    grid_in = lax.all_to_all(
        jnp.take(grid_latent, wanted, axis=0), "patch", split_axis=0, concat_axis=0, tiled=True
    )
    grid_proj = jnp.dot(grid_in, w1_grid, preferred_element_type=jnp.float32).astype(jnp.bfloat16)
    mesh_in = jnp.take(mesh_latent, mesh_rows, axis=0)
    before = (
        grid_proj.astype(jnp.float32)
        + jnp.dot(mesh_in, w1_mesh, preferred_element_type=jnp.float32)
        + bias_one
    )
    activation, derivative = swish_parts(before)
    hidden = activation.astype(jnp.bfloat16)
    out_grad = jnp.where(
        live_mask[:, None], jnp.take(mesh_cotangent, mesh_rows, axis=0), jnp.zeros((), jnp.bfloat16)
    )
    hid_grad = jnp.dot(out_grad, w2.T, preferred_element_type=jnp.float32)
    pre_grad = (hid_grad * derivative).astype(jnp.bfloat16)
    edge_grid = jnp.dot(pre_grad, w1_grid.T, preferred_element_type=jnp.float32).astype(
        jnp.bfloat16
    )
    returned = lax.all_to_all(edge_grid, "patch", split_axis=0, concat_axis=0, tiled=True)
    grid_part = jnp.dot(grid_in.T, pre_grad, preferred_element_type=jnp.float32)
    grid_grad = jax.ops.segment_sum(
        returned.astype(jnp.float32), wanted, num_segments=grid_latent.shape[0]
    )
    node_sum = jax.ops.segment_sum(
        pre_grad.astype(jnp.float32), mesh_rows, num_segments=mesh_latent.shape[0]
    )
    mesh_grad = jnp.dot(node_sum, w1_mesh.T.astype(jnp.float32), precision=lax.Precision.HIGHEST)
    mesh_part = jnp.dot(mesh_in.T, pre_grad, preferred_element_type=jnp.float32)
    second_part = jnp.dot(hidden.T, out_grad, preferred_element_type=jnp.float32)
    bias_part = jnp.sum(pre_grad.astype(jnp.float32), axis=0)
    totals = lax.psum((grid_part, mesh_part, second_part, bias_part), "patch")
    norm_scale = 1.0 / math.sqrt(members * slot_count)
    return (
        grid_grad,
        mesh_grad,
        totals[0] * norm_scale,
        totals[1] * norm_scale,
        totals[2] * norm_scale,
        totals[3] * norm_scale,
    )


def solution(mesh):
    return jax.shard_map(
        body,
        mesh=mesh,
        in_specs=(
            P("patch", None),
            P("patch", None),
            P("patch", None),
            P("patch"),
            P("patch"),
            P("patch", None),
            P(),
            P(),
            P(),
            P(),
        ),
        out_specs=(P("patch", None), P("patch", None), P(), P(), P(), P()),
        check_vma=False,
    )
```

profile of v0, /device:TPU:0, one launch (start us, length us, event | category | flops | bytes accessed | tf_op | source)
XLA Modules:
  0.0 210.8 jit_solution(12706923728167780505)
XLA Ops:
  7.2 0.9 all_to_all.20
  8.1 14.3 %all_to_all.30 = s32[32,12,1]{1,2,0:T(1,128)S(1)} all-to-all(s32[32,12,1]{1,2,0:T(1,128)S(1)} %bitcast.18), channel_id=1, replica_groups=mesh['patch'=32] {'patch'}, dimensions={0} | all-to-all | bytes 3072 | tf_op jit(solution)/shard_map/all_to_all | solution.py:32
  22.6 4.8 %gather_fusion = bf16[384,512]{1,0:T(8,128)(2,1)S(1)} fusion(bf16[4096,512]{1,0:T(8,128)(2,1)} %param.12, s32[1024]{0:T(1024)S(1)} %pad_clamp_fusion), kind=kCustom, calls=%fused_computation.2 | custom fusion | bytes 787968 | tf_op jit(solution)/shard_map/jit(_take)/gather | solution.py:34
  27.5 0.9 broadcast_select_fusion
  28.5 2.6 %all-to-all-start.1 = ((bf16[32,12,512]{2,1,0:T(8,128)(2,1)}), bf16[32,12,512]{2,1,0:T(8,128)(2,1)S(1)}, u32[]{:S(2)}, u32[]{:S(2)}) async-start(bf16[32,12,512]{2,1,0:T(8,128)(2,1)} %broadcast_select_fusion), calls=%async_computation.1 | async-start | bytes 1048576 | tf_op jit(solution)/shard_map/all_to_all | solution.py:33
  31.1 0.7 compare_select_fusion.2
  31.8 2.1 gather_fusion.2
  33.9 2.1 gather_fusion.1
  36.2 10.5 %all-to-all-done.1 = bf16[32,12,512]{2,1,0:T(8,128)(2,1)S(1)} async-done(((bf16[32,12,512]{2,1,0:T(8,128)(2,1)}), bf16[32,12,512]{2,1,0:T(8,128)(2,1)S(1)}, u32[]{:S(2)}, u32[]{:S(2)}) %all-to-all-start.1) | async-done | bytes 393248 | tf_op jit(solution)/shard_map/all_to_all | solution.py:33
  47.6 1.6 convert_reduce_fusion
  49.2 1.4 fusion.16
  50.7 1.5 fusion.10
  52.2 1.6 fusion.7
  54.2 0.9 all_to_all.25
  55.1 2.9 %all-to-all-start.2 = ((bf16[32,12,512]{2,1,0:T(8,128)(2,1)}), bf16[32,12,512]{2,1,0:T(8,128)(2,1)S(1)}, u32[]{:S(2)}, u32[]{:S(2)}) async-start(bf16[32,12,512]{2,1,0:T(8,128)(2,1)} %all_to_all.25), calls=%async_computation.2 | async-start | bytes 1048576 | tf_op jit(solution)/shard_map/all_to_all | solution.py:53
  58.5 0.7 reduce.7
  59.3 3.0 %scatter_custom_fusion.1 = f32[320,512]{1,0:T(8,128)S(1)} fusion(s32[384]{0:T(512)S(1)} %copy-done.4, bf16[384,512]{1,0:T(8,128)(2,1)S(1)} %get-tuple-element.11, f32[]{:T(128)} %constant.10.clone.1), kind=kCustom, calls=%fused_computation.15 | custom fusion | flops 393216 | bytes 1048580 | tf_op jit(solution)/shard_map/scatter-add | solution.py:58
  62.4 40.9 %psum.31 = f32[512]{0:T(512)S(1)} all-reduce(f32[512]{0:T(512)S(1)} %get-tuple-element.10), channel_id=1, replica_groups=mesh['patch'=32] {'patch'}, use_global_device_ids=true, to_apply=%region_6.8 | all-reduce | flops 512 | bytes 4096 | tf_op jit(solution)/shard_map/psum | solution.py:65
  103.3 0.6 broadcast_multiply_fusion.3
  103.8 1.6 fusion.15
  105.5 6.7 %scatter_custom_fusion = f32[4096,512]{1,0:T(8,128)} fusion(s32[384]{0:T(512)S(1)} %reshape.109, f32[384,512]{1,0:T(8,128)S(1)} %reshape.111, f32[]{:T(128)} %constant.10.clone.1), kind=kCustom, calls=%fused_computation.5 | custom fusion | flops 196608 | bytes 8388612 | tf_op jit(solution)/shard_map/scatter-add | solution.py:55
  112.2 86.4 %all-reduce.3.cloned.1.call-done = (f32[512,512]{1,0:T(8,128)}, f32[512,512]{1,0:T(8,128)}, f32[512,512]{1,0:T(8,128)}) async-done(((f32[512,512]{1,0:T(8,128)}, f32[512,512]{1,0:T(8,128)}, f32[512,512]{1,0:T(8,128)}), (f32[512,512]{1,0:T(8,128)}, f32[512,512]{1,0:T(8,128)}, f32[512,512]{1,0:T(8,128)})) %all-reduce.3.cloned.1.call-update) | async-done | bytes 3145744 | tf_op jit(solution)/shard_map/psum | solution.py:65
  198.6 2.3 %broadcast_multiply_fusion.2 = f32[512,512]{1,0:T(8,128)} fusion(f32[512,512]{1,0:T(8,128)} %get-tuple-element.7), kind=kLoop, calls=%fused_computation.21 | loop fusion | flops 262144 | bytes 2097152 | tf_op jit(solution)/shard_map/mul | solution.py:70
  200.9 3.1 %broadcast_multiply_fusion = (f32[512,512]{1,0:T(8,128)}, f32[512,512]{1,0:T(8,128)}) fusion(f32[512,512]{1,0:T(8,128)} %get-tuple-element.9, f32[512,512]{1,0:T(8,128)} %get-tuple-element.8), kind=kLoop, calls=%fused_computation.19 | loop fusion | flops 524288 | bytes 4194304 | tf_op jit(solution)/shard_map/mul | solution.py:72
  (33 shorter events, 2.5 us)
Async XLA Ops:
  7.2 39.6 %copy-start = (bf16[512,512]{1,0:T(8,128)(2,1)S(1)}, bf16[512,512]{1,0:T(8,128)(2,1)}, u32[]{:S(2)}) copy-start(bf16[512,512]{1,0:T(8,128)(2,1)} %param.18) | copy-start | bytes 1572868
  7.2 29.0 %copy-start.4 = (s32[384]{0:T(512)S(1)}, s32[384]{0:T(512)}, u32[]{:S(2)}) copy-start(s32[384]{0:T(512)} %param.16) | copy-start | bytes 4612
  7.2 24.6 %copy-start.1 = (bf16[320,512]{1,0:T(8,128)(2,1)S(1)}, bf16[320,512]{1,0:T(8,128)(2,1)}, u32[]{:S(2)}) copy-start(bf16[320,512]{1,0:T(8,128)(2,1)} %param.13) | copy-start | bytes 983044
  7.2 26.7 %copy-start.2 = (bf16[320,512]{1,0:T(8,128)(2,1)S(1)}, bf16[320,512]{1,0:T(8,128)(2,1)}, u32[]{:S(2)}) copy-start(bf16[320,512]{1,0:T(8,128)(2,1)} %param.14) | copy-start | bytes 983044
  7.2 28.8 %copy-start.6 = (s32[1,32]{1,0:T(1,128)S(1)}, s32[1,32]{1,0:T(1,128)}, u32[]{:S(2)}) copy-start(s32[1,32]{1,0:T(1,128)} %param.17) | copy-start | bytes 388
  7.2 39.9 %copy-start.3 = (bf16[512,512]{1,0:T(8,128)(2,1)S(1)}, bf16[512,512]{1,0:T(8,128)(2,1)}, u32[]{:S(2)}) copy-start(bf16[512,512]{1,0:T(8,128)(2,1)} %param.19) | copy-start | bytes 1572868
  7.2 39.9 %copy-start.5 = (f32[512]{0:T(512)S(1)}, f32[512]{0:T(512)}, u32[]{:S(2)}) copy-start(f32[512]{0:T(512)} %param.20) | copy-start | bytes 6148
  28.5 18.2 %all-to-all-start.1 = ((bf16[32,12,512]{2,1,0:T(8,128)(2,1)}), bf16[32,12,512]{2,1,0:T(8,128)(2,1)S(1)}, u32[]{:S(2)}, u32[]{:S(2)}) async-start(bf16[32,12,512]{2,1,0:T(8,128)(2,1)} %broadcast_select_fusion), calls=%async_computation.1 | async-start | bytes 1048576 | tf_op jit(solution)/shard_map/all_to_all | solution.py:33
  31.1 167.5 %all-reduce.3.cloned.1.call-start = ((), (), s32[]{:S(2)}) async-start(), calls=%async_computation.3 | async-start | bytes 6291456 | tf_op jit(solution)/shard_map/psum | solution.py:65
  55.1 50.3 %all-to-all-start.2 = ((bf16[32,12,512]{2,1,0:T(8,128)(2,1)}), bf16[32,12,512]{2,1,0:T(8,128)(2,1)S(1)}, u32[]{:S(2)}, u32[]{:S(2)}) async-start(bf16[32,12,512]{2,1,0:T(8,128)(2,1)} %all_to_all.25), calls=%async_computation.2 | async-start | bytes 1048576 | tf_op jit(solution)/shard_map/all_to_all | solution.py:53
Sparse Core Ops, SparseCore 0:
  53.9 144.5 all-reduce.2
where the time goes:
time: 211 us
  waiting for transfers between devices  96.9 us (46%)
  blocking collectives  55.2 us (26%)
  other arithmetic  18.2 us (9%)
  between operations  14.3 us (7%)
  local copies, waits for them, and re-layouts  11.8 us (6%)
  matrix products  8.91 us (4%)
  starting transfers between devices  5.53 us (3%)
    psum x1, waiting for transfers between devices, body(): totals = lax.psum((grid_part, mesh_part, second_part, bias_part), 'patch')  86.4 us
    psum x1, blocking collectives, body(): totals = lax.psum((grid_part, mesh_part, second_part, bias_part), 'patch')  40.9 us
    all_to_all x1, blocking collectives, body(): lax.all_to_all(grid_rows, 'patch', split_axis=0, concat_axis=0, tiled=True)  14.3 us
    all_to_all x1, waiting for transfers between devices, body(): lax.all_to_all(jnp.take(grid_latent, wanted, axis=0), 'patch', split_axis...  10.5 us
    scatter-add x1, other arithmetic, body(): jax.ops.segment_sum(returned.astype(jnp.float32), wanted, num_segments=gr...  6.72 us
    gather x2, local copies, waits for them, and re-layouts, body(): jnp.take(grid_latent, wanted, axis=0)  4.9 us
  transfers between devices with their start and end apart: 3, of which 2 were waited for; matrix products, arithmetic and copies ran while one was open for 9% of the time, Pallas kernels for 0%

commit v1 on v0

v1 whole, which is shorter than its diff:
```python
import functools
import math

import jax
import jax.numpy as jnp
from jax import lax
from jax.experimental import pallas as pl
from jax.experimental.pallas import tpu as pltpu
from jax.sharding import PartitionSpec as P

SUB = 8
HALF = SUB // 2
F32 = jnp.float32
BF16 = jnp.bfloat16
WHOLE = pl.BlockSpec(memory_space=pltpu.VMEM)
GRANT = pltpu.CompilerParams(vmem_limit_bytes=24 << 20)


def dot(left, right, dims=((1,), (0,))):
    return lax.dot_general(left, right, (dims, ((), ())), preferred_element_type=F32)


def near(value):
    return pltpu.with_memory_space_constraint(value, pltpu.VMEM)


def call(kernel, outs, scratch=(), flops=0, leaves=False):
    make = jax.ShapeDtypeStruct if leaves else pltpu.VMEM
    built = pl.pallas_call(
        kernel,
        out_shape=[make(shape, dtype) for shape, dtype in outs],
        scratch_shapes=list(scratch),
        compiler_params=GRANT,
        cost_estimate=pl.CostEstimate(flops=flops, transcendentals=0, bytes_accessed=0),
    )
    return lambda *values: built(*map(near, values))


def column(index):
    members, capacity = index.shape
    middle = members // 2
    lane = lax.broadcasted_iota(jnp.int32, (members, SUB, capacity), 2)
    row = lax.broadcasted_iota(jnp.int32, (members, SUB, capacity), 1)
    spread = jnp.broadcast_to(index[:, None, :], (members, SUB, capacity))
    head = jnp.sum(jnp.where(lane == row, spread, 0).astype(F32), axis=2, keepdims=True)
    upper = row[:middle] < HALF
    chosen = jnp.where(upper, spread[:middle], spread[middle:])
    wanted = jnp.where(upper, row[:middle] + SUB, row[:middle] + HALF)
    tail = jnp.sum(jnp.where(lane[:middle] == wanted, chosen, 0).astype(F32), axis=2, keepdims=True)
    return jnp.concatenate(
        (head.reshape(members * SUB, 1), tail.reshape(middle * SUB, 1)), axis=0
    ).astype(jnp.int32)


def lanes(index):
    col = column(index).astype(F32)
    return jnp.transpose(jnp.broadcast_to(col, (col.shape[0], 128)))[:1].astype(jnp.int32)


def pick(col, start, size):
    at = lax.broadcasted_iota(jnp.int32, (col.shape[0], size), 1) + start
    return jnp.where(at == col, 1.0, 0.0).astype(BF16)


def pack(rows, members):
    width = rows.shape[1]
    middle = members // 2
    head = rows[: members * SUB].reshape(members, SUB, width)
    tail = rows[members * SUB :].reshape(middle, SUB, width)
    left, right = tail[:, :, : width // 2], tail[:, :, width // 2 :]
    upper = lax.broadcasted_iota(jnp.int32, left.shape, 1) < HALF
    first = jnp.where(upper, left, pltpu.roll(right, HALF, 1))
    second = jnp.where(upper, pltpu.roll(left, HALF, 1), right)
    return head, jnp.concatenate((first, second), axis=0)


def unpack(packed, width):
    members = packed.shape[0]
    middle = members // 2
    head = packed[:, :, :width].reshape(members * SUB, width)
    first = packed[:middle, :, width : width + width // 2]
    second = packed[middle:, :, width : width + width // 2]
    upper = lax.broadcasted_iota(jnp.int32, first.shape, 1) < HALF
    left = jnp.where(upper, first, pltpu.roll(second, HALF, 1))
    right = jnp.where(upper, pltpu.roll(first, HALF, 1), second)
    tail = jnp.concatenate((left, right), axis=2).reshape(middle * SUB, width)
    return jnp.concatenate((head, tail), axis=0)


def gather_kernel(index_ref, table_ref, out_ref):
    members = index_ref.shape[0]
    width = table_ref.shape[1]
    col = column(index_ref[...])
    step = min(512, table_ref.shape[0])
    total = None
    for start in range(0, table_ref.shape[0], step):
        part = dot(pick(col, start, step), table_ref[start : start + step, :])
        total = part if total is None else total + part
    head, tail = pack(total, members)
    out_ref[:, :, :width] = head.astype(BF16)
    out_ref[:, :, width:] = tail.astype(BF16)


def mesh_kernel(
    rows_ref, live_ref, latent_ref, cot_ref, w1_ref, w2_ref, bias_ref, in_ref, grad_ref, base_ref, hid_ref
):
    nodes = latent_ref.shape[0]
    mesh_in = dot(pick(column(rows_ref[...]), 0, nodes), latent_ref[...]).astype(BF16)
    out_grad = dot(pick(column(live_ref[...]), 0, nodes), cot_ref[...]).astype(BF16)
    in_ref[...] = mesh_in
    grad_ref[...] = out_grad
    base_ref[...] = dot(mesh_in, w1_ref[...]) + bias_ref[...]
    hid_ref[...] = dot(out_grad, w2_ref[...], ((1,), (1,)))


def edge_kernel(
    got_ref, base_ref, hid_ref, mesh_ref, grad_ref, w1_ref, sent_ref, kept_ref, pre_ref, full_ref
):
    width = mesh_ref.shape[1]
    half = sent_ref.shape[1]
    core = lax.rem(lax.axis_index("patch"), 2)
    grid_in = unpack(got_ref[...].astype(F32), width).astype(BF16)
    before = dot(grid_in, w1_ref[...]).astype(BF16).astype(F32) + base_ref[...]
    logistic = jax.nn.sigmoid(before)
    hidden = (before * logistic).astype(BF16)
    derivative = logistic * (1.0 + before * (1.0 - logistic))
    pre = (hid_ref[...] * derivative).astype(BF16)
    pre_ref[...] = pre
    across = ((0,), (0,))
    full_ref[0] = dot(grid_in, pre, across)
    full_ref[1] = dot(mesh_ref[...], pre, across)
    full_ref[2] = dot(hidden, grad_ref[...], across)
    for which in range(3):
        away = pl.multiple_of((1 - core) * half, half)
        home = pl.multiple_of(core * half, half)
        sent_ref[which] = full_ref[which, pl.ds(away, half), :].astype(BF16)
        kept_ref[which] = full_ref[which, pl.ds(home, half), :]


def return_kernel(pre_ref, w1_ref, out_ref):
    members = out_ref.shape[0]
    width = pre_ref.shape[1]
    pre = pre_ref[...]
    head, tail = pack(dot(pre, w1_ref[...], ((1,), (1,))), members)
    out_ref[:, :, :width] = head.astype(BF16)
    out_ref[:, :, width : width + width // 2] = tail.astype(BF16)
    bias = jnp.sum(pre.astype(F32), axis=0, keepdims=True)
    high = bias.astype(BF16).astype(F32)
    low = bias - high
    at = lax.broadcasted_iota(jnp.int32, (SUB, 128), 0)
    tile = jnp.zeros((SUB, 128), F32)
    for part in range(width // 128):
        block = slice(part * 128, part * 128 + 128)
        tile = jnp.where(at == part, high[:, block], tile)
        tile = jnp.where(at == part + width // 128, low[:, block], tile)
    out_ref[:, :, width + width // 2 :] = jnp.broadcast_to(tile[None], (members, SUB, 128)).astype(
        BF16
    )


def scatter_kernel(index_ref, came_ref, out_ref, rows_ref, flat_ref):
    step = pl.program_id(0)
    size, width = out_ref.shape

    @pl.when(step == 0)
    def _():
        flat_ref[...] = jnp.broadcast_to(lanes(index_ref[...]), flat_ref.shape)
        rows_ref[...] = unpack(came_ref[...].astype(F32), width).astype(BF16)

    at = lax.broadcasted_iota(jnp.int32, (size, rows_ref.shape[0]), 0) + step * size
    chosen = jnp.where(at == flat_ref[:1], 1.0, 0.0).astype(BF16)
    out_ref[...] = dot(chosen, rows_ref[...])


def bias_kernel(scale, came_ref, out_ref):
    width = out_ref.shape[1]
    tile = jnp.sum(came_ref[:, :, width + width // 2 :].astype(F32), axis=0)
    for part in range(width // 128):
        low = part + width // 128
        out_ref[:, part * 128 : part * 128 + 128] = (
            tile[part : part + 1] + tile[low : low + 1]
        ) * scale


def node_kernel(rows_ref, pre_ref, w1_ref, out_ref):
    nodes = out_ref.shape[0]
    flat = lanes(rows_ref[...])
    at = lax.broadcasted_iota(jnp.int32, (nodes, flat.shape[1]), 0)
    sums = dot(jnp.where(at == flat, 1.0, 0.0).astype(BF16), pre_ref[...])
    total = None
    for _ in range(3):
        piece = sums.astype(BF16)
        part = dot(piece, w1_ref[...], ((1,), (1,)))
        total = part if total is None else total + part
        sums = sums - piece.astype(F32)
    out_ref[...] = total


def place(stride, size):
    return lax.rem(lax.div(lax.axis_index("patch"), stride), size)


def fold(own, came, stride, size):
    count, rows, width = own.shape
    cut = rows // size

    def kernel(*refs):
        inputs, outputs = refs[: 1 + len(came)], refs[1 + len(came) :]
        here = place(stride, size) if size > 1 else 0
        for k, out_ref in enumerate(outputs):
            start = pl.multiple_of((here ^ k) * cut, cut) if size > 1 else 0
            total = sum(ref[:, pl.ds(start, cut), :].astype(F32) for ref in inputs)
            out_ref[...] = total.astype(out_ref.dtype)

    types = [F32 if k == 0 and size > 1 else BF16 for k in range(size)]
    if cut % 16 == 0:
        return call(kernel, [((count, cut, width), dtype) for dtype in types])(own, *came)
    total = own.astype(F32) + sum(part.astype(F32) for part in came)
    here = place(stride, size) if size > 1 else 0
    return [
        lax.dynamic_slice_in_dim(total, (here ^ k) * cut, cut, axis=1).astype(dtype)
        for k, dtype in enumerate(types)
    ]


def join(pieces, stride):
    count, cut, width = pieces[0].shape
    size = len(pieces)

    def kernel(*refs):
        here = place(stride, size)
        for k in range(size):
            start = pl.multiple_of((here ^ k) * cut, cut)
            refs[-1][:, pl.ds(start, cut), :] = refs[k][...]

    if cut % 16 == 0:
        return call(kernel, [((count, cut * size, width), BF16)])(*pieces)[0]
    order = jnp.arange(size, dtype=jnp.int32) ^ place(stride, size)
    return jnp.take(jnp.stack(pieces, axis=1), order, axis=1).reshape(count, cut * size, width)


def send(value, step, members):
    return lax.ppermute(value, "patch", [(i, i ^ step) for i in range(members)])


def final_kernel(scale, stride, size, *refs):
    pieces, outputs = refs[: 2 * size], refs[2 * size :]
    core = lax.rem(lax.axis_index("patch"), 2)
    here = place(stride, size)
    cut = pieces[0].shape[1]
    for side in range(2):
        base = (core if side == 0 else 1 - core) * (cut * size)
        for k in range(size):
            start = pl.multiple_of(base + (here ^ k) * cut, cut)
            for which, out_ref in enumerate(outputs):
                out_ref[pl.ds(start, cut), :] = pieces[side * size + k][which].astype(F32) * scale


def body(
    grid_latent,
    mesh_latent,
    mesh_cotangent,
    grid_rows,
    mesh_rows,
    counts,
    w1_grid,
    w1_mesh,
    bias_one,
    w2,
):
    members = lax.axis_size("patch")
    slots = grid_rows.shape[0]
    capacity = slots // members
    width = grid_latent.shape[1]
    nodes = mesh_latent.shape[0]
    points = grid_latent.shape[0]
    if capacity != SUB + HALF or members & (members - 1):
        raise ValueError("slot layout")
    scale = 1.0 / math.sqrt(members * slots)
    steps = []
    rest, stride = members // 2, 2
    while rest > 1:
        size = 4 if rest % 4 == 0 else 2
        steps.append((stride, size))
        rest, stride = rest // size, stride * size

    swap = functools.partial(
        lax.all_to_all, axis_name="patch", split_axis=0, concat_axis=0, tiled=True
    )
    wanted = swap(grid_rows.reshape(members, capacity))
    rows2d = mesh_rows.reshape(members, capacity)
    slot = jnp.arange(capacity, dtype=jnp.int32)[None, :]
    live2d = jnp.where(slot < counts[0][:, None], rows2d, -1)
    packed = (members, SUB, width + width // 2)
    found = call(gather_kernel, [(packed, BF16)], flops=2 * slots * points * width)(
        wanted, grid_latent
    )[0]
    got = swap(found)
    flat = (slots, width)
    mesh_in, out_grad, base, hid = call(
        mesh_kernel, [(flat, BF16), (flat, BF16), (flat, F32), (flat, F32)], flops=8 * slots * width**2
    )(rows2d, live2d, mesh_latent, mesh_cotangent, w1_mesh, w2, bias_one.reshape(1, width))
    halves = (3, width // 2, width)
    sent, kept, pre = call(
        edge_kernel,
        [(halves, BF16), (halves, F32), (flat, BF16)],
        [pltpu.VMEM((3, width, width), F32)],
        flops=8 * slots * width**2,
    )(got, base, hid, mesh_in, out_grad, w1_grid)

    came = [send(sent, 1, members)]
    own = kept
    for stride, size in steps:
        own, *away = fold(own, came, stride, size)
        came = [send(part, k * stride, members) for k, part in enumerate(away, 1)]
    pieces = [fold(own, came, 1, 1)[0]]
    for position, (stride, size) in reversed(list(enumerate(steps))):
        share = pieces[0]
        pieces = [share] + [send(share, k * stride, members) for k in range(1, size)]
        if position > 0:
            pieces = [join(pieces, stride)]
    stride, size = steps[0]
    others = [send(piece, 1, members) for piece in pieces]
    grads = call(
        functools.partial(final_kernel, scale, stride, size), [((width, width), F32)] * 3, leaves=True
    )(*pieces, *others)

    leaving = call(
        return_kernel, [((members, SUB, 2 * width - width // 2 + 128), BF16)], flops=2 * slots * width**2
    )(pre, w1_grid)[0]
    returned = swap(leaving)
    block = min(512, points)
    grid_grad = pl.pallas_call(
        scatter_kernel,
        out_shape=jax.ShapeDtypeStruct((points, width), F32),
        grid=(points // block,),
        compiler_params=GRANT,
        in_specs=[WHOLE, WHOLE],
        out_specs=pl.BlockSpec((block, width), lambda i: (i, 0)),
        scratch_shapes=[pltpu.VMEM(flat, BF16), pltpu.VMEM((SUB, slots), jnp.int32)],
        cost_estimate=pl.CostEstimate(
            flops=2 * slots * points * width, transcendentals=0, bytes_accessed=4 * points * width
        ),
    )(near(wanted), near(returned))
    bias_grad = call(functools.partial(bias_kernel, scale), [((1, width), F32)], leaves=True)(returned)[0]
    mesh_grad = call(node_kernel, [((nodes, width), F32)], flops=8 * nodes * width**2, leaves=True)(
        rows2d, pre, w1_mesh
    )[0]
    return (grid_grad, mesh_grad, *grads, bias_grad.reshape(width))


def solution(mesh):
    rows, line = P("patch", None), P("patch")
    return jax.shard_map(
        body,
        mesh=mesh,
        in_specs=(rows, rows, rows, line, line, rows, P(), P(), P(), P()),
        out_specs=(rows, rows, P(), P(), P(), P()),
        check_vma=False,
    )
```

time: 211 us -> 104 us (0.49)
  waiting for transfers between devices: 96.9 us -> 32.3 us
  blocking collectives: 55.2 us -> 14.3 us
  Pallas kernels: 0 us -> 19.5 us
  other arithmetic: 18.2 us -> 0.07 us
  starting transfers between devices: 5.53 us -> 21.7 us
  between operations: 14.3 us -> 0.8 us
  matrix products: 8.91 us -> 0 us
  local copies, waits for them, and re-layouts: 11.8 us -> 14.4 us
    psum x1 -> x0, waiting for transfers between devices: 86.4 us -> none  [body(): totals = lax.psum((grid_part, mesh_part, second_part, bias_part), 'patch')]
    psum x1 -> x0, blocking collectives: 40.9 us -> none  [body(): totals = lax.psum((grid_part, mesh_part, second_part, bias_part), 'patch')]
    ppermute x0 -> x17, waiting for transfers between devices: none -> 26.1 us  [send(): return lax.ppermute(value, 'patch', [(i, i ^ step) for i in range(members)])]
    pallas_call x0 -> x12, Pallas kernels: none -> 19.5 us  [the longest x11 13.1 us: call(): return lambda *values: built(*map(near, values))]
    ppermute x0 -> x17, starting transfers between devices: none -> 16.5 us  [send(): return lax.ppermute(value, 'patch', [(i, i ^ step) for i in range(members)])]
    unnamed x14 -> x36, local copies, waits for them, and re-layouts: 0.04 us -> 13.5 us
    scatter-add x2 -> x0, other arithmetic: 9.76 us -> none  [the longest x1 6.72 us: body(): jax.ops.segment_sum(returned.astype(jnp.float32), wanted, num_segments=gr...]
    gather x4 -> x0, local copies, waits for them, and re-layouts: 9.03 us -> none  [the longest x2 4.9 us: body(): jnp.take(grid_latent, wanted, axis=0)]
  transfers between devices with their start and end apart: 3 -> 19, of which waited for: 2 -> 10; matrix products, arithmetic and copies ran while one was open for 9% -> 0% of each run, Pallas kernels for 0% -> 12%
where the time goes in v1:
time: 104 us; the launch traced here: 103 us
  waiting for transfers between devices  32.3 us (31%)
  starting transfers between devices  21.7 us (21%)
  Pallas kernels  19.5 us (19%)
  local copies, waits for them, and re-layouts  14.4 us (14%)
  blocking collectives  14.3 us (14%)
    ppermute x17, waiting for transfers between devices, send(): return lax.ppermute(value, 'patch', [(i, i ^ step) for i in range(members)])  26.1 us
    ppermute x17, starting transfers between devices, send(): return lax.ppermute(value, 'patch', [(i, i ^ step) for i in range(members)])  16.5 us
    all_to_all x1, blocking collectives, body(): wanted = swap(grid_rows.reshape(members, capacity))  14.3 us
    unnamed x36, local copies, waits for them, and re-layouts  13.5 us
    pallas_call x11, Pallas kernels, call(): return lambda *values: built(*map(near, values))  13.1 us
    pallas_call x1, Pallas kernels, body(): pl.pallas_call(scatter_kernel, out_shape=jax.ShapeDtypeStruct((points, wi...  6.44 us
    all_to_all x1, waiting for transfers between devices, body(): got = swap(found)  6.26 us
    all_to_all x1, starting transfers between devices, body(): returned = swap(leaving)  2.6 us
  transfers between devices with their start and end apart: 19, of which 10 were waited for; matrix products, arithmetic and copies ran while one was open for 0% of the time, Pallas kernels for 12%

profile of v1, /device:TPU:0, one launch (start us, length us, event | category | flops | bytes accessed | tf_op | source)
XLA Modules:
  0.0 103.2 jit_solution(15054715242415766249)
XLA Ops:
  1.5 14.3 %all_to_all.21 = s32[32,1,12]{2,1,0:T(1,128)S(1)} all-to-all(s32[32,1,12]{2,1,0:T(1,128)S(1)} %bitcast.8), channel_id=1, replica_groups=mesh['patch'=32] {'patch'}, dimensions={0} | all-to-all | bytes 3072 | tf_op jit(solution)/shard_map/all_to_all | solution.py:290
  15.8 2.2 %copy-done.9 = bf16[4096,512]{1,0:T(8,128)(2,1)S(1)} copy-done((bf16[4096,512]{1,0:T(8,128)(2,1)S(1)}, bf16[4096,512]{1,0:T(8,128)(2,1)}, u32[]{:S(2)}) %copy-start.9) | copy-done | bytes 4194328
  18.0 2.8 %shard_map.145 = bf16[32,8,768]{2,1,0:T(8,128)(2,1)} custom-call(s32[32,12]{1,0:T(8,128)S(1)} %bitcast.5, bf16[4096,512]{1,0:T(8,128)(2,1)S(1)} %copy-done.9), custom_call_target="tpu_custom_call" | custom-call | flops 1610612736 | tf_op jit(solution)/shard_map/pallas_call | solution.py:36
  20.7 2.6 %all-to-all-start.1 = ((bf16[32,8,768]{2,1,0:T(8,128)(2,1)}), bf16[32,8,768]{2,1,0:T(8,128)(2,1)S(1)}, u32[]{:S(2)}, u32[]{:S(2)}) async-start(bf16[32,8,768]{2,1,0:T(8,128)(2,1)} %shard_map.145), calls=%async_computation.1 | async-start | bytes 786432 | tf_op jit(solution)/shard_map/all_to_all | solution.py:298
  30.3 6.3 %all-to-all-done.1.got_ref = bf16[32,8,768]{2,1,0:T(8,128)(2,1)S(1)} async-done(((bf16[32,8,768]{2,1,0:T(8,128)(2,1)}), bf16[32,8,768]{2,1,0:T(8,128)(2,1)S(1)}, u32[]{:S(2)}, u32[]{:S(2)}) %all-to-all-start.1) | async-done | bytes 393248 | tf_op jit(solution)/shard_map/all_to_all | solution.py:298
  39.7 2.9 %shard_map.147 = (bf16[3,256,512]{2,1,0:T(8,128)(2,1)}, f32[3,256,512]{2,1,0:T(8,128)S(1)}, bf16[384,512]{1,0:T(8,128)(2,1)S(1)}) custom-call(bf16[32,8,768]{2,1,0:T(8,128)(2,1)S(1)} %all-to-all-done.1.got_ref, f32[384,512]{1,0:T(8,128)S(1)} %get-tuple-element.24.base_ref, f32[384,512]{1,0:T(8,128)S(1)} %copy-done.2, bf16[384,512]{1,0:T(8,128)(2,1)S(1)} %copy-done.4, ...), custom_call_target="tpu_custom_call" | custom-call | flops 805306368 | tf_op jit(solution)/shard_map/pallas_call | solution.py:36
  44.6 2.6 %all-to-all-start.2 = ((bf16[32,8,896]{2,1,0:T(8,128)(2,1)}), bf16[32,8,896]{2,1,0:T(8,128)(2,1)S(1)}, u32[]{:S(2)}, u32[]{:S(2)}) async-start(bf16[32,8,896]{2,1,0:T(8,128)(2,1)} %shard_map.148), calls=%async_computation.2 | async-start | bytes 917504 | tf_op jit(solution)/shard_map/all_to_all | solution.py:331
  47.3 1.8 %collective-permute-start.1 = (bf16[3,64,512]{2,1,0:T(8,128)(2,1)S(1)}, bf16[3,64,512]{2,1,0:T(8,128)(2,1)S(1)}, u32[]{:S(2)}, u32[]{:S(2)}) collective-permute-start(bf16[3,64,512]{2,1,0:T(8,128)(2,1)S(1)} %get-tuple-element.32), channel_id=1, source_target_pairs={{0,2},{1,3},{2,0},{3,1},{4,6},{5,7},{6,4},{7,5},{8,10},{9,11},{10,... | collective-permute-start | bytes 589832 | tf_op jit(solution)/shard_map/ppermute | solution.py:243
  49.1 1.5 %collective-permute-start.2 = (bf16[3,64,512]{2,1,0:T(8,128)(2,1)S(1)}, bf16[3,64,512]{2,1,0:T(8,128)(2,1)S(1)}, u32[]{:S(2)}, u32[]{:S(2)}) collective-permute-start(bf16[3,64,512]{2,1,0:T(8,128)(2,1)S(1)} %get-tuple-element.33), channel_id=1, source_target_pairs={{0,4},{1,5},{2,6},{3,7},{4,0},{5,1},{6,2},{7,3},{8,12},{9,13},{10,... | collective-permute-start | bytes 589832 | tf_op jit(solution)/shard_map/ppermute | solution.py:243
  50.9 8.4 %collective-permute-done.1.refs_1_ = bf16[3,64,512]{2,1,0:T(8,128)(2,1)S(1)} collective-permute-done((bf16[3,64,512]{2,1,0:T(8,128)(2,1)S(1)}, bf16[3,64,512]{2,1,0:T(8,128)(2,1)S(1)}, u32[]{:S(2)}, u32[]{:S(2)}) %collective-permute-start.1) | collective-permute-done | bytes 196640 | tf_op jit(solution)/shard_map/ppermute | solution.py:243
  59.3 4.9 %collective-permute-done.3.refs_3_ = bf16[3,64,512]{2,1,0:T(8,128)(2,1)S(1)} collective-permute-done((bf16[3,64,512]{2,1,0:T(8,128)(2,1)S(1)}, bf16[3,64,512]{2,1,0:T(8,128)(2,1)S(1)}, u32[]{:S(2)}, u32[]{:S(2)}) %collective-permute-start.3) | collective-permute-done | bytes 196640 | tf_op jit(solution)/shard_map/ppermute | solution.py:243
  64.3 1.5 %collective-permute-start.4 = (bf16[3,16,512]{2,1,0:T(8,128)(2,1)S(1)}, bf16[3,16,512]{2,1,0:T(8,128)(2,1)S(1)}, u32[]{:S(2)}, u32[]{:S(2)}) collective-permute-start(bf16[3,16,512]{2,1,0:T(8,128)(2,1)S(1)} %get-tuple-element.36), channel_id=1, source_target_pairs={{0,8},{1,9},{2,10},{3,11},{4,12},{5,13},{6,14},{7,15},{8,0},{9,1},... | collective-permute-start | bytes 147464 | tf_op jit(solution)/shard_map/ppermute | solution.py:243
  65.8 2.4 %collective-permute-start.5 = (bf16[3,16,512]{2,1,0:T(8,128)(2,1)S(1)}, bf16[3,16,512]{2,1,0:T(8,128)(2,1)S(1)}, u32[]{:S(2)}, u32[]{:S(2)}) collective-permute-start(bf16[3,16,512]{2,1,0:T(8,128)(2,1)S(1)} %get-tuple-element.37), channel_id=1, source_target_pairs={{0,16},{1,17},{2,18},{3,19},{4,20},{5,21},{6,22},{7,23},{8,24},{9,... | collective-permute-start | bytes 147464 | tf_op jit(solution)/shard_map/ppermute | solution.py:243
  68.7 2.7 %collective-permute-done.5.refs_2_ = bf16[3,16,512]{2,1,0:T(8,128)(2,1)S(1)} collective-permute-done((bf16[3,16,512]{2,1,0:T(8,128)(2,1)S(1)}, bf16[3,16,512]{2,1,0:T(8,128)(2,1)S(1)}, u32[]{:S(2)}, u32[]{:S(2)}) %collective-permute-start.5) | collective-permute-done | bytes 49184 | tf_op jit(solution)/shard_map/ppermute | solution.py:243
  71.4 2.7 %collective-permute-done.6.refs_3_ = bf16[3,16,512]{2,1,0:T(8,128)(2,1)S(1)} collective-permute-done((bf16[3,16,512]{2,1,0:T(8,128)(2,1)S(1)}, bf16[3,16,512]{2,1,0:T(8,128)(2,1)S(1)}, u32[]{:S(2)}, u32[]{:S(2)}) %collective-permute-start.6) | collective-permute-done | bytes 49184 | tf_op jit(solution)/shard_map/ppermute | solution.py:243
  74.9 3.7 %collective-permute-start.7 = (bf16[3,16,512]{2,1,0:T(8,128)(2,1)S(1)}, bf16[3,16,512]{2,1,0:T(8,128)(2,1)S(1)}, u32[]{:S(2)}, u32[]{:S(2)}) collective-permute-start(bf16[3,16,512]{2,1,0:T(8,128)(2,1)S(1)} %shard_map.153.refs_0_), channel_id=1, source_target_pairs={{0,8},{1,9},{2,10},{3,11},{4,12},{5,13},{6,14},{7,15},{8,0},{9,1},... | collective-permute-start | bytes 147464 | tf_op jit(solution)/shard_map/ppermute | solution.py:243
  78.7 1.6 %collective-permute-done.9.refs_3_ = bf16[3,16,512]{2,1,0:T(8,128)(2,1)S(1)} collective-permute-done((bf16[3,16,512]{2,1,0:T(8,128)(2,1)S(1)}, bf16[3,16,512]{2,1,0:T(8,128)(2,1)S(1)}, u32[]{:S(2)}, u32[]{:S(2)}) %collective-permute-start.9) | collective-permute-done | bytes 49184 | tf_op jit(solution)/shard_map/ppermute | solution.py:243
  81.7 1.4 %collective-permute-start.11 = (bf16[3,64,512]{2,1,0:T(8,128)(2,1)S(1)}, bf16[3,64,512]{2,1,0:T(8,128)(2,1)S(1)}, u32[]{:S(2)}, u32[]{:S(2)}) collective-permute-start(bf16[3,64,512]{2,1,0:T(8,128)(2,1)S(1)} %shard_map.154.refs_0_), channel_id=1, source_target_pairs={{0,4},{1,5},{2,6},{3,7},{4,0},{5,1},{6,2},{7,3},{8,12},{9,13},{10,... | collective-permute-start | bytes 589832 | tf_op jit(solution)/shard_map/ppermute | solution.py:243
  83.1 1.4 %collective-permute-start.10 = (bf16[3,64,512]{2,1,0:T(8,128)(2,1)S(1)}, bf16[3,64,512]{2,1,0:T(8,128)(2,1)S(1)}, u32[]{:S(2)}, u32[]{:S(2)}) collective-permute-start(bf16[3,64,512]{2,1,0:T(8,128)(2,1)S(1)} %shard_map.154.refs_0_), channel_id=1, source_target_pairs={{0,2},{1,3},{2,0},{3,1},{4,6},{5,7},{6,4},{7,5},{8,10},{9,11},{10,... | collective-permute-start | bytes 589832 | tf_op jit(solution)/shard_map/ppermute | solution.py:243
  84.5 3.7 %collective-permute-done.12.refs_3_ = bf16[3,64,512]{2,1,0:T(8,128)(2,1)S(1)} collective-permute-done((bf16[3,64,512]{2,1,0:T(8,128)(2,1)S(1)}, bf16[3,64,512]{2,1,0:T(8,128)(2,1)S(1)}, u32[]{:S(2)}, u32[]{:S(2)}) %collective-permute-start.12) | collective-permute-done | bytes 196640 | tf_op jit(solution)/shard_map/ppermute | solution.py:243
  88.2 1.4 %collective-permute-done.11.refs_2_ = bf16[3,64,512]{2,1,0:T(8,128)(2,1)S(1)} collective-permute-done((bf16[3,64,512]{2,1,0:T(8,128)(2,1)S(1)}, bf16[3,64,512]{2,1,0:T(8,128)(2,1)S(1)}, u32[]{:S(2)}, u32[]{:S(2)}) %collective-permute-start.11) | collective-permute-done | bytes 196640 | tf_op jit(solution)/shard_map/ppermute | solution.py:243
  92.1 2.1 %shard_map.150 = f32[320,512]{1,0:T(8,128)} custom-call(s32[32,12]{1,0:T(8,128)S(1)} %reshape.26.rows_ref, bf16[384,512]{1,0:T(8,128)(2,1)S(1)} %copy-done.8, bf16[512,512]{1,0:T(8,128)(2,1)S(1)} %copy-done.12), custom_call_target="tpu_custom_call" | custom-call | flops 671088640 | tf_op jit(solution)/shard_map/pallas_call | solution.py:36
  94.8 6.4 %shard_map.149 = f32[4096,512]{1,0:T(8,128)} custom-call(s32[32,12]{1,0:T(8,128)S(1)} %bitcast.6, bf16[32,8,896]{2,1,0:T(8,128)(2,1)S(1)} %all-to-all-done.2.came_ref), custom_call_target="tpu_custom_call" | custom-call | flops 1610612736 | bytes 8388608 | tf_op jit(solution)/shard_map/pallas_call | solution.py:333
  101.3 1.9 %shard_map.155 = (f32[512,512]{1,0:T(8,128)}, f32[512,512]{1,0:T(8,128)}, f32[512,512]{1,0:T(8,128)}) custom-call(bf16[3,64,512]{2,1,0:T(8,128)(2,1)S(1)} %shard_map.154.refs_0_, bf16[3,64,512]{2,1,0:T(8,128)(2,1)S(1)} %collective-permute-done.10.refs_1_, bf16[3,64,512]{2,1,0:T(8,128)(2,1)S(1)} %collective-permute-done.11.refs_2_, ...), custom_call_target="tpu_custom_call" | custom-call | tf_op jit(solution)/shard_map/pallas_call | solution.py:36
  (66 shorter events, 19.2 us)
Async XLA Ops:
  0.6 22.7 %copy-start.16 = (s32[384]{0:T(512)S(1)}, s32[384]{0:T(512)}, u32[]{:S(2)}) copy-start(s32[384]{0:T(512)} %param.14) | copy-start | bytes 4612
  0.6 22.8 %copy-start.17 = (s32[1,32]{1,0:T(1,128)S(1)}, s32[1,32]{1,0:T(1,128)}, u32[]{:S(2)}) copy-start(s32[1,32]{1,0:T(1,128)} %param.15) | copy-start | bytes 388
  0.7 22.9 %copy-start.15 = (f32[512]{0:T(512)S(1)}, f32[512]{0:T(512)}, u32[]{:S(2)}) copy-start(f32[512]{0:T(512)} %param.18) | copy-start | bytes 6148
  18.0 5.6 %copy-start.13 = (bf16[320,512]{1,0:T(8,128)(2,1)S(1)}, bf16[320,512]{1,0:T(8,128)(2,1)}, u32[]{:S(2)}) copy-start(bf16[320,512]{1,0:T(8,128)(2,1)} %latent_ref.1) | copy-start | bytes 983044
  18.0 18.6 %copy-start = (bf16[512,512]{1,0:T(8,128)(2,1)S(1)}, bf16[512,512]{1,0:T(8,128)(2,1)}, u32[]{:S(2)}) copy-start(bf16[512,512]{1,0:T(8,128)(2,1)} %w1_ref.6) | copy-start | bytes 1572868
  20.7 15.8 %all-to-all-start.1 = ((bf16[32,8,768]{2,1,0:T(8,128)(2,1)}), bf16[32,8,768]{2,1,0:T(8,128)(2,1)S(1)}, u32[]{:S(2)}, u32[]{:S(2)}) async-start(bf16[32,8,768]{2,1,0:T(8,128)(2,1)} %shard_map.145), calls=%async_computation.1 | async-start | bytes 786432 | tf_op jit(solution)/shard_map/all_to_all | solution.py:298
  42.6 4.5 %collective-permute-start = (bf16[3,256,512]{2,1,0:T(8,128)(2,1)}, bf16[3,256,512]{2,1,0:T(8,128)(2,1)S(1)}, u32[]{:S(2)}, u32[]{:S(2)}) collective-permute-start(bf16[3,256,512]{2,1,0:T(8,128)(2,1)} %get-tuple-element.30), channel_id=1, source_target_pairs={{0,1},{1,0},{2,3},{3,2},{4,5},{5,4},{6,7},{7,6},{8,9},{9,8},{10,11... | collective-permute-start | bytes 2359304 | tf_op jit(solution)/shard_map/ppermute | solution.py:243
  44.6 49.7 %all-to-all-start.2 = ((bf16[32,8,896]{2,1,0:T(8,128)(2,1)}), bf16[32,8,896]{2,1,0:T(8,128)(2,1)S(1)}, u32[]{:S(2)}, u32[]{:S(2)}) async-start(bf16[32,8,896]{2,1,0:T(8,128)(2,1)} %shard_map.148), calls=%async_computation.2 | async-start | bytes 917504 | tf_op jit(solution)/shard_map/all_to_all | solution.py:331
  47.3 11.9 %collective-permute-start.1 = (bf16[3,64,512]{2,1,0:T(8,128)(2,1)S(1)}, bf16[3,64,512]{2,1,0:T(8,128)(2,1)S(1)}, u32[]{:S(2)}, u32[]{:S(2)}) collective-permute-start(bf16[3,64,512]{2,1,0:T(8,128)(2,1)S(1)} %get-tuple-element.32), channel_id=1, source_target_pairs={{0,2},{1,3},{2,0},{3,1},{4,6},{5,7},{6,4},{7,5},{8,10},{9,11},{10,... | collective-permute-start | bytes 589832 | tf_op jit(solution)/shard_map/ppermute | solution.py:243
  49.1 10.2 %collective-permute-start.2 = (bf16[3,64,512]{2,1,0:T(8,128)(2,1)S(1)}, bf16[3,64,512]{2,1,0:T(8,128)(2,1)S(1)}, u32[]{:S(2)}, u32[]{:S(2)}) collective-permute-start(bf16[3,64,512]{2,1,0:T(8,128)(2,1)S(1)} %get-tuple-element.33), channel_id=1, source_target_pairs={{0,4},{1,5},{2,6},{3,7},{4,0},{5,1},{6,2},{7,3},{8,12},{9,13},{10,... | collective-permute-start | bytes 589832 | tf_op jit(solution)/shard_map/ppermute | solution.py:243
  50.6 13.6 %collective-permute-start.3 = (bf16[3,64,512]{2,1,0:T(8,128)(2,1)S(1)}, bf16[3,64,512]{2,1,0:T(8,128)(2,1)S(1)}, u32[]{:S(2)}, u32[]{:S(2)}) collective-permute-start(bf16[3,64,512]{2,1,0:T(8,128)(2,1)S(1)} %get-tuple-element.34), channel_id=1, source_target_pairs={{0,6},{1,7},{2,4},{3,5},{4,2},{5,3},{6,0},{7,1},{8,14},{9,15},{10,... | collective-permute-start | bytes 589832 | tf_op jit(solution)/shard_map/ppermute | solution.py:243
  64.3 4.5 %collective-permute-start.4 = (bf16[3,16,512]{2,1,0:T(8,128)(2,1)S(1)}, bf16[3,16,512]{2,1,0:T(8,128)(2,1)S(1)}, u32[]{:S(2)}, u32[]{:S(2)}) collective-permute-start(bf16[3,16,512]{2,1,0:T(8,128)(2,1)S(1)} %get-tuple-element.36), channel_id=1, source_target_pairs={{0,8},{1,9},{2,10},{3,11},{4,12},{5,13},{6,14},{7,15},{8,0},{9,1},... | collective-permute-start | bytes 147464 | tf_op jit(solution)/shard_map/ppermute | solution.py:243
  65.8 5.6 %collective-permute-start.5 = (bf16[3,16,512]{2,1,0:T(8,128)(2,1)S(1)}, bf16[3,16,512]{2,1,0:T(8,128)(2,1)S(1)}, u32[]{:S(2)}, u32[]{:S(2)}) collective-permute-start(bf16[3,16,512]{2,1,0:T(8,128)(2,1)S(1)} %get-tuple-element.37), channel_id=1, source_target_pairs={{0,16},{1,17},{2,18},{3,19},{4,20},{5,21},{6,22},{7,23},{8,24},{9,... | collective-permute-start | bytes 147464 | tf_op jit(solution)/shard_map/ppermute | solution.py:243
  68.3 5.9 %collective-permute-start.6 = (bf16[3,16,512]{2,1,0:T(8,128)(2,1)S(1)}, bf16[3,16,512]{2,1,0:T(8,128)(2,1)S(1)}, u32[]{:S(2)}, u32[]{:S(2)}) collective-permute-start(bf16[3,16,512]{2,1,0:T(8,128)(2,1)S(1)} %get-tuple-element.38), channel_id=1, source_target_pairs={{0,24},{1,25},{2,26},{3,27},{4,28},{5,29},{6,30},{7,31},{8,16},{9,... | collective-permute-start | bytes 147464 | tf_op jit(solution)/shard_map/ppermute | solution.py:243
  74.2 6.1 %collective-permute-start.9 = (bf16[3,16,512]{2,1,0:T(8,128)(2,1)S(1)}, bf16[3,16,512]{2,1,0:T(8,128)(2,1)S(1)}, u32[]{:S(2)}, u32[]{:S(2)}) collective-permute-start(bf16[3,16,512]{2,1,0:T(8,128)(2,1)S(1)} %shard_map.153.refs_0_), channel_id=1, source_target_pairs={{0,24},{1,25},{2,26},{3,27},{4,28},{5,29},{6,30},{7,31},{8,16},{9,... | collective-permute-start | bytes 147464 | tf_op jit(solution)/shard_map/ppermute | solution.py:243
  74.8 6.0 %collective-permute-start.8 = (bf16[3,16,512]{2,1,0:T(8,128)(2,1)S(1)}, bf16[3,16,512]{2,1,0:T(8,128)(2,1)S(1)}, u32[]{:S(2)}, u32[]{:S(2)}) collective-permute-start(bf16[3,16,512]{2,1,0:T(8,128)(2,1)S(1)} %shard_map.153.refs_0_), channel_id=1, source_target_pairs={{0,16},{1,17},{2,18},{3,19},{4,20},{5,21},{6,22},{7,23},{8,24},{9,... | collective-permute-start | bytes 147464 | tf_op jit(solution)/shard_map/ppermute | solution.py:243
  74.9 5.9 %collective-permute-start.7 = (bf16[3,16,512]{2,1,0:T(8,128)(2,1)S(1)}, bf16[3,16,512]{2,1,0:T(8,128)(2,1)S(1)}, u32[]{:S(2)}, u32[]{:S(2)}) collective-permute-start(bf16[3,16,512]{2,1,0:T(8,128)(2,1)S(1)} %shard_map.153.refs_0_), channel_id=1, source_target_pairs={{0,8},{1,9},{2,10},{3,11},{4,12},{5,13},{6,14},{7,15},{8,0},{9,1},... | collective-permute-start | bytes 147464 | tf_op jit(solution)/shard_map/ppermute | solution.py:243
  80.9 7.2 %collective-permute-start.12 = (bf16[3,64,512]{2,1,0:T(8,128)(2,1)S(1)}, bf16[3,64,512]{2,1,0:T(8,128)(2,1)S(1)}, u32[]{:S(2)}, u32[]{:S(2)}) collective-permute-start(bf16[3,64,512]{2,1,0:T(8,128)(2,1)S(1)} %shard_map.154.refs_0_), channel_id=1, source_target_pairs={{0,6},{1,7},{2,4},{3,5},{4,2},{5,3},{6,0},{7,1},{8,14},{9,15},{10,... | collective-permute-start | bytes 589832 | tf_op jit(solution)/shard_map/ppermute | solution.py:243
  81.7 7.8 %collective-permute-start.11 = (bf16[3,64,512]{2,1,0:T(8,128)(2,1)S(1)}, bf16[3,64,512]{2,1,0:T(8,128)(2,1)S(1)}, u32[]{:S(2)}, u32[]{:S(2)}) collective-permute-start(bf16[3,64,512]{2,1,0:T(8,128)(2,1)S(1)} %shard_map.154.refs_0_), channel_id=1, source_target_pairs={{0,4},{1,5},{2,6},{3,7},{4,0},{5,1},{6,2},{7,3},{8,12},{9,13},{10,... | collective-permute-start | bytes 589832 | tf_op jit(solution)/shard_map/ppermute | solution.py:243
  83.1 6.4 %collective-permute-start.10 = (bf16[3,64,512]{2,1,0:T(8,128)(2,1)S(1)}, bf16[3,64,512]{2,1,0:T(8,128)(2,1)S(1)}, u32[]{:S(2)}, u32[]{:S(2)}) collective-permute-start(bf16[3,64,512]{2,1,0:T(8,128)(2,1)S(1)} %shard_map.154.refs_0_), channel_id=1, source_target_pairs={{0,2},{1,3},{2,0},{3,1},{4,6},{5,7},{6,4},{7,5},{8,10},{9,11},{10,... | collective-permute-start | bytes 589832 | tf_op jit(solution)/shard_map/ppermute | solution.py:243
  84.5 16.8 %collective-permute-start.13 = (bf16[3,64,512]{2,1,0:T(8,128)(2,1)S(1)}, bf16[3,64,512]{2,1,0:T(8,128)(2,1)S(1)}, u32[]{:S(2)}, u32[]{:S(2)}) collective-permute-start(bf16[3,64,512]{2,1,0:T(8,128)(2,1)S(1)} %shard_map.154.refs_0_), channel_id=1, source_target_pairs={{0,1},{1,0},{2,3},{3,2},{4,5},{5,4},{6,7},{7,6},{8,9},{9,8},{10,11... | collective-permute-start | bytes 589832 | tf_op jit(solution)/shard_map/ppermute | solution.py:243
  88.2 13.1 %collective-permute-start.16 = (bf16[3,64,512]{2,1,0:T(8,128)(2,1)S(1)}, bf16[3,64,512]{2,1,0:T(8,128)(2,1)S(1)}, u32[]{:S(2)}, u32[]{:S(2)}) collective-permute-start(bf16[3,64,512]{2,1,0:T(8,128)(2,1)S(1)} %collective-permute-done.12.refs_3_), channel_id=1, source_target_pairs={{0,1},{1,0},{2,3},{3,2},{4,5},{5,4},{6,7},{7,6},{8,9},{9,8},{10,11... | collective-permute-start | bytes 589832 | tf_op jit(solution)/shard_map/ppermute | solution.py:243
  89.5 11.7 %collective-permute-start.15 = (bf16[3,64,512]{2,1,0:T(8,128)(2,1)S(1)}, bf16[3,64,512]{2,1,0:T(8,128)(2,1)S(1)}, u32[]{:S(2)}, u32[]{:S(2)}) collective-permute-start(bf16[3,64,512]{2,1,0:T(8,128)(2,1)S(1)} %collective-permute-done.11.refs_2_), channel_id=1, source_target_pairs={{0,1},{1,0},{2,3},{3,2},{4,5},{5,4},{6,7},{7,6},{8,9},{9,8},{10,11... | collective-permute-start | bytes 589832 | tf_op jit(solution)/shard_map/ppermute | solution.py:243
  89.6 11.7 %collective-permute-start.14 = (bf16[3,64,512]{2,1,0:T(8,128)(2,1)S(1)}, bf16[3,64,512]{2,1,0:T(8,128)(2,1)S(1)}, u32[]{:S(2)}, u32[]{:S(2)}) collective-permute-start(bf16[3,64,512]{2,1,0:T(8,128)(2,1)S(1)} %collective-permute-done.10.refs_1_), channel_id=1, source_target_pairs={{0,1},{1,0},{2,3},{3,2},{4,5},{5,4},{6,7},{7,6},{8,9},{9,8},{10,11... | collective-permute-start | bytes 589832 | tf_op jit(solution)/shard_map/ppermute | solution.py:243
  (13 other events, 13.5 us)

commit v2 on v1

--- a/solution.py
+++ b/solution.py
@@ -8,12 +8,14 @@
 from jax.experimental.pallas import tpu as pltpu
 from jax.sharding import PartitionSpec as P
 
+
 SUB = 8
 HALF = SUB // 2
 F32 = jnp.float32
 BF16 = jnp.bfloat16
 WHOLE = pl.BlockSpec(memory_space=pltpu.VMEM)
-GRANT = pltpu.CompilerParams(vmem_limit_bytes=24 << 20)
+FAR = pl.BlockSpec(memory_space=pltpu.HBM)
+GRANT = pltpu.CompilerParams(vmem_limit_bytes=30 << 20)
 
 
 def dot(left, right, dims=((1,), (0,))):
@@ -24,16 +26,22 @@
     return pltpu.with_memory_space_constraint(value, pltpu.VMEM)
 
 
-def call(kernel, outs, scratch=(), flops=0, leaves=False):
+def far(value):
+    return pltpu.with_memory_space_constraint(value, pltpu.HBM)
+
+
+def call(kernel, outs, scratch=(), flops=0, leaves=False, specs=None):
     make = jax.ShapeDtypeStruct if leaves else pltpu.VMEM
     built = pl.pallas_call(
         kernel,
+        **({} if specs is None else {"in_specs": specs}),
         out_shape=[make(shape, dtype) for shape, dtype in outs],
         scratch_shapes=list(scratch),
         compiler_params=GRANT,
         cost_estimate=pl.CostEstimate(flops=flops, transcendentals=0, bytes_accessed=0),
     )
-    return lambda *values: built(*map(near, values))
+    places = [near] * 99 if specs is None else [far if spec is FAR else near for spec in specs]
+    return lambda *values: built(*(place(value) for place, value in zip(places, values)))
 
 
 def column(index):
@@ -87,57 +95,79 @@
     return jnp.concatenate((head, tail), axis=0)
 
 
-def gather_kernel(index_ref, table_ref, out_ref):
+def gather_kernel(index_ref, table_ref, out_ref, held_ref, sems):
     members = index_ref.shape[0]
     width = table_ref.shape[1]
+    count, step, _ = held_ref.shape
+    copies = [
+        pltpu.make_async_copy(table_ref.at[pl.ds(k * step, step), :], held_ref.at[k], sems.at[k])
+        for k in range(count)
+    ]
+    for copy in copies:
+        copy.start()
     col = column(index_ref[...])
-    step = min(512, table_ref.shape[0])
     total = None
-    for start in range(0, table_ref.shape[0], step):
-        part = dot(pick(col, start, step), table_ref[start : start + step, :])
+    for k, copy in enumerate(copies):
+        chosen = pick(col, k * step, step)
+        copy.wait()
+        part = dot(chosen, held_ref[k])
         total = part if total is None else total + part
     head, tail = pack(total, members)
     out_ref[:, :, :width] = head.astype(BF16)
     out_ref[:, :, width:] = tail.astype(BF16)
 
 
-def mesh_kernel(
-    rows_ref, live_ref, latent_ref, cot_ref, w1_ref, w2_ref, bias_ref, in_ref, grad_ref, base_ref, hid_ref
+def edge_kernel(
+    got_ref,
+    rows_ref,
+    live_ref,
+    latent_ref,
+    cot_ref,
+    w1m_ref,
+    w2_ref,
+    bias_ref,
+    w1g_ref,
+    sent_ref,
+    kept_ref,
+    pre_ref,
+    full_ref,
+    latent_vmem,
+    cot_vmem,
+    sems,
 ):
-    nodes = latent_ref.shape[0]
-    mesh_in = dot(pick(column(rows_ref[...]), 0, nodes), latent_ref[...]).astype(BF16)
-    out_grad = dot(pick(column(live_ref[...]), 0, nodes), cot_ref[...]).astype(BF16)
-    in_ref[...] = mesh_in
-    grad_ref[...] = out_grad
-    base_ref[...] = dot(mesh_in, w1_ref[...]) + bias_ref[...]
-    hid_ref[...] = dot(out_grad, w2_ref[...], ((1,), (1,)))
-
-
-def edge_kernel(
-    got_ref, base_ref, hid_ref, mesh_ref, grad_ref, w1_ref, sent_ref, kept_ref, pre_ref, full_ref
-):
-    width = mesh_ref.shape[1]
+    nodes, width = latent_ref.shape
+    load_latent = pltpu.make_async_copy(latent_ref, latent_vmem, sems.at[0])
+    load_cot = pltpu.make_async_copy(cot_ref, cot_vmem, sems.at[1])
+    load_latent.start()
+    load_cot.start()
     half = sent_ref.shape[1]
     core = lax.rem(lax.axis_index("patch"), 2)
     grid_in = unpack(got_ref[...].astype(F32), width).astype(BF16)
-    before = dot(grid_in, w1_ref[...]).astype(BF16).astype(F32) + base_ref[...]
+    grid_proj = dot(grid_in, w1g_ref[...]).astype(BF16).astype(F32)
+    picked = pick(column(rows_ref[...]), 0, nodes)
+    live = pick(column(live_ref[...]), 0, nodes)
+    load_latent.wait()
+    mesh_in = dot(picked, latent_vmem[...]).astype(BF16)
+    load_cot.wait()
+    out_grad = dot(live, cot_vmem[...]).astype(BF16)
+    before = grid_proj + dot(mesh_in, w1m_ref[...]) + bias_ref[...]
     logistic = jax.nn.sigmoid(before)
     hidden = (before * logistic).astype(BF16)
     derivative = logistic * (1.0 + before * (1.0 - logistic))
-    pre = (hid_ref[...] * derivative).astype(BF16)
+    pre = (dot(out_grad, w2_ref[...], ((1,), (1,))) * derivative).astype(BF16)
     pre_ref[...] = pre
     across = ((0,), (0,))
     full_ref[0] = dot(grid_in, pre, across)
-    full_ref[1] = dot(mesh_ref[...], pre, across)
-    full_ref[2] = dot(hidden, grad_ref[...], across)
+    full_ref[1] = dot(mesh_in, pre, across)
+    full_ref[2] = dot(hidden, out_grad, across)
+    away = pl.multiple_of((1 - core) * half, half)
+    home = pl.multiple_of(core * half, half)
     for which in range(3):
-        away = pl.multiple_of((1 - core) * half, half)
-        home = pl.multiple_of(core * half, half)
         sent_ref[which] = full_ref[which, pl.ds(away, half), :].astype(BF16)
         kept_ref[which] = full_ref[which, pl.ds(home, half), :]
 
 
-def return_kernel(pre_ref, w1_ref, out_ref):
+def return_kernel(pre_ref, w1_ref, after_ref, out_ref):
     members = out_ref.shape[0]
     width = pre_ref.shape[1]
     pre = pre_ref[...]
@@ -158,7 +188,7 @@
     )
 
 
-def scatter_kernel(index_ref, came_ref, out_ref, rows_ref, flat_ref):
+def scatter_kernel(index_ref, came_ref, after_ref, out_ref, rows_ref, flat_ref):
     step = pl.program_id(0)
     size, width = out_ref.shape
 
@@ -182,7 +212,7 @@
         ) * scale
 
 
-def node_kernel(rows_ref, pre_ref, w1_ref, out_ref):
+def node_kernel(rows_ref, pre_ref, w1_ref, after_ref, out_ref):
     nodes = out_ref.shape[0]
     flat = lanes(rows_ref[...])
     at = lax.broadcasted_iota(jnp.int32, (nodes, flat.shape[1]), 0)
@@ -292,27 +322,62 @@
     slot = jnp.arange(capacity, dtype=jnp.int32)[None, :]
     live2d = jnp.where(slot < counts[0][:, None], rows2d, -1)
     packed = (members, SUB, width + width // 2)
-    found = call(gather_kernel, [(packed, BF16)], flops=2 * slots * points * width)(
-        wanted, grid_latent
-    )[0]
+    count = next(k for k in (8, 4, 2, 1) if points % (k * SUB) == 0)
+    found = pl.pallas_call(
+        gather_kernel,
+        out_shape=pltpu.VMEM(packed, BF16),
+        in_specs=[WHOLE, FAR],
+        out_specs=WHOLE,
+        scratch_shapes=[
+            pltpu.VMEM((count, points // count, width), BF16),
+            pltpu.SemaphoreType.DMA((count,)),
+        ],
+        compiler_params=GRANT,
+        cost_estimate=pl.CostEstimate(
+            flops=2 * slots * points * width, transcendentals=0, bytes_accessed=2 * points * width
+        ),
+    )(near(wanted), far(grid_latent))
     got = swap(found)
     flat = (slots, width)
-    mesh_in, out_grad, base, hid = call(
-        mesh_kernel, [(flat, BF16), (flat, BF16), (flat, F32), (flat, F32)], flops=8 * slots * width**2
-    )(rows2d, live2d, mesh_latent, mesh_cotangent, w1_mesh, w2, bias_one.reshape(1, width))
     halves = (3, width // 2, width)
     sent, kept, pre = call(
         edge_kernel,
         [(halves, BF16), (halves, F32), (flat, BF16)],
-        [pltpu.VMEM((3, width, width), F32)],
-        flops=8 * slots * width**2,
-    )(got, base, hid, mesh_in, out_grad, w1_grid)
+        [
+            pltpu.VMEM((3, width, width), F32),
+            pltpu.VMEM((nodes, width), BF16),
+            pltpu.VMEM((nodes, width), BF16),
+            pltpu.SemaphoreType.DMA((2,)),
+        ],
+        flops=14 * slots * width**2,
+        specs=[WHOLE, WHOLE, WHOLE, FAR, FAR, WHOLE, WHOLE, WHOLE, WHOLE],
+    )(
+        got,
+        rows2d,
+        live2d,
+        mesh_latent,
+        mesh_cotangent,
+        w1_mesh,
+        w2,
+        bias_one.reshape(1, width),
+        w1_grid,
+    )
 
     came = [send(sent, 1, members)]
     own = kept
+    after = None
     for stride, size in steps:
         own, *away = fold(own, came, stride, size)
         came = [send(part, k * stride, members) for k, part in enumerate(away, 1)]
+        after = own if after is None else after
+
+    wide = (members, SUB, 2 * width - width // 2 + 128)
+    leaving = call(return_kernel, [(wide, BF16)], flops=2 * slots * width**2)(pre, w1_grid, after)[0]
+    returned = swap(leaving)
+    mesh_grad = call(
+        node_kernel, [((nodes, width), F32)], flops=8 * nodes * width**2, leaves=True
+    )(rows2d, pre, w1_mesh, after)[0]
+
     pieces = [fold(own, came, 1, 1)[0]]
     for position, (stride, size) in reversed(list(enumerate(steps))):
         share = pieces[0]
@@ -320,31 +385,25 @@
         if position > 0:
             pieces = [join(pieces, stride)]
     stride, size = steps[0]
-    others = [send(piece, 1, members) for piece in pieces]
-    grads = call(
-        functools.partial(final_kernel, scale, stride, size), [((width, width), F32)] * 3, leaves=True
-    )(*pieces, *others)
-
-    leaving = call(
-        return_kernel, [((members, SUB, 2 * width - width // 2 + 128), BF16)], flops=2 * slots * width**2
-    )(pre, w1_grid)[0]
-    returned = swap(leaving)
     block = min(512, points)
     grid_grad = pl.pallas_call(
         scatter_kernel,
         out_shape=jax.ShapeDtypeStruct((points, width), F32),
         grid=(points // block,),
         compiler_params=GRANT,
-        in_specs=[WHOLE, WHOLE],
+        in_specs=[WHOLE, WHOLE, WHOLE],
         out_specs=pl.BlockSpec((block, width), lambda i: (i, 0)),
         scratch_shapes=[pltpu.VMEM(flat, BF16), pltpu.VMEM((SUB, slots), jnp.int32)],
         cost_estimate=pl.CostEstimate(
             flops=2 * slots * points * width, transcendentals=0, bytes_accessed=4 * points * width
         ),
-    )(near(wanted), near(returned))
-    bias_grad = call(functools.partial(bias_kernel, scale), [((1, width), F32)], leaves=True)(returned)[0]
-    mesh_grad = call(node_kernel, [((nodes, width), F32)], flops=8 * nodes * width**2, leaves=True)(
-        rows2d, pre, w1_mesh
+    )(near(wanted), near(returned), near(pieces[0]))
+    others = [send(piece, 1, members) for piece in pieces]
+    grads = call(
+        functools.partial(final_kernel, scale, stride, size), [((width, width), F32)] * 3, leaves=True
+    )(*pieces, *others)
+    bias_grad = call(functools.partial(bias_kernel, scale), [((1, width), F32)], leaves=True)(
+        returned
     )[0]
     return (grid_grad, mesh_grad, *grads, bias_grad.reshape(width))
 

time: 104 us -> 100 us (0.962)
  local copies, waits for them, and re-layouts: 14.4 us -> 1.02 us
  waiting for transfers between devices: 32.3 us -> 41.5 us
    unnamed x36 -> x12, local copies, waits for them, and re-layouts: 13.5 us -> 0.03 us
    all_to_all x1, waiting for transfers between devices: 6.26 us -> 13.1 us  [body(): got = swap(found)]
    ppermute x17, waiting for transfers between devices: 26.1 us -> 28.5 us  [send(): return lax.ppermute(value, 'patch', [(i, i ^ step) for i in range(members)])]
    pallas_call x11 -> x10, Pallas kernels: 13.1 us -> 14 us  [the longest x9 9.89 us: call(): built(*(place(value) for place, value in zip(places, values)))]
  transfers between devices with their start and end apart: 19 -> 19, of which waited for: 10 -> 11; matrix products, arithmetic and copies ran while one was open for 0% -> 0% of each run, Pallas kernels for 12% -> 4%
where the time goes in v2:
time: 100 us
  waiting for transfers between devices  41.5 us (42%)
  starting transfers between devices  21.8 us (22%)
  Pallas kernels  20.5 us (20%)
  blocking collectives  14.3 us (14%)
  local copies, waits for them, and re-layouts  1.02 us (1%)
    ppermute x17, waiting for transfers between devices, send(): return lax.ppermute(value, 'patch', [(i, i ^ step) for i in range(members)])  28.5 us
    ppermute x17, starting transfers between devices, send(): return lax.ppermute(value, 'patch', [(i, i ^ step) for i in range(members)])  16.6 us
    all_to_all x1, blocking collectives, body(): wanted = swap(grid_rows.reshape(members, capacity))  14.3 us
    all_to_all x1, waiting for transfers between devices, body(): got = swap(found)  13.1 us
    pallas_call x9, Pallas kernels, call(): built(*(place(value) for place, value in zip(places, values)))  9.89 us
    pallas_call x1, Pallas kernels, body(): pl.pallas_call(scatter_kernel, out_shape=jax.ShapeDtypeStruct((points, wi...  6.44 us
    pallas_call x1, Pallas kernels, body(): pl.pallas_call(gather_kernel, out_shape=pltpu.VMEM(packed, BF16), in_spec...  4.12 us
    all_to_all x1, starting transfers between devices, body(): got = swap(found)  2.61 us
  transfers between devices with their start and end apart: 19, of which 11 were waited for; matrix products, arithmetic and copies ran while one was open for 0% of the time, Pallas kernels for 4%

profile of v2, /device:TPU:0, one launch (start us, length us, event | category | flops | bytes accessed | tf_op | source)
XLA Modules:
  0.0 100.0 jit_solution(6741504499223956868)
XLA Ops:
  1.6 14.3 %all_to_all.21 = s32[32,1,12]{2,1,0:T(1,128)S(1)} all-to-all(s32[32,1,12]{2,1,0:T(1,128)S(1)} %bitcast.8), channel_id=1, replica_groups=mesh['patch'=32] {'patch'}, dimensions={0} | all-to-all | bytes 3072 | tf_op jit(solution)/shard_map/all_to_all | solution.py:320
  15.9 4.1 %shard_map.145 = bf16[32,8,768]{2,1,0:T(8,128)(2,1)} custom-call(s32[32,12]{1,0:T(8,128)S(1)} %bitcast.5, bf16[4096,512]{1,0:T(8,128)(2,1)} %table_ref.1), custom_call_target="tpu_custom_call" | custom-call | flops 1610612736 | bytes 4194304 | tf_op jit(solution)/shard_map/pallas_call | solution.py:326
  20.0 2.6 %all-to-all-start.1 = ((bf16[32,8,768]{2,1,0:T(8,128)(2,1)}), bf16[32,8,768]{2,1,0:T(8,128)(2,1)S(1)}, u32[]{:S(2)}, u32[]{:S(2)}) async-start(bf16[32,8,768]{2,1,0:T(8,128)(2,1)} %shard_map.145), calls=%async_computation.1 | async-start | bytes 786432 | tf_op jit(solution)/shard_map/all_to_all | solution.py:340
  22.8 13.1 %all-to-all-done.1.got_ref = bf16[32,8,768]{2,1,0:T(8,128)(2,1)S(1)} async-done(((bf16[32,8,768]{2,1,0:T(8,128)(2,1)}), bf16[32,8,768]{2,1,0:T(8,128)(2,1)S(1)}, u32[]{:S(2)}, u32[]{:S(2)}) %all-to-all-start.1) | async-done | bytes 393248 | tf_op jit(solution)/shard_map/all_to_all | solution.py:340
  35.9 3.8 %shard_map.146 = (bf16[3,256,512]{2,1,0:T(8,128)(2,1)S(1)}, f32[3,256,512]{2,1,0:T(8,128)S(1)}, bf16[384,512]{1,0:T(8,128)(2,1)S(1)}) custom-call(bf16[32,8,768]{2,1,0:T(8,128)(2,1)S(1)} %all-to-all-done.1.got_ref, s32[32,12]{1,0:T(8,128)S(1)} %reshape.26.rows_ref, s32[32,12]{1,0:T(8,128)S(1)} %fusion.live_ref, bf16[320,512]{1,0:T(8,128)(2,1)} %latent_ref.1, ...), custom_call_target="tpu_custom_call" | custom-call | flops 1409286144 | tf_op jit(solution)/shard_map/pallas_call | solution.py:44
  39.8 2.3 %collective-permute-done.refs_1_ = bf16[3,256,512]{2,1,0:T(8,128)(2,1)S(1)} collective-permute-done((bf16[3,256,512]{2,1,0:T(8,128)(2,1)S(1)}, bf16[3,256,512]{2,1,0:T(8,128)(2,1)S(1)}, u32[]{:S(2)}, u32[]{:S(2)}) %collective-permute-start) | collective-permute-done | bytes 786464 | tf_op jit(solution)/shard_map/ppermute | solution.py:273
  43.4 2.6 %all-to-all-start.2 = ((bf16[32,8,896]{2,1,0:T(8,128)(2,1)}), bf16[32,8,896]{2,1,0:T(8,128)(2,1)S(1)}, u32[]{:S(2)}, u32[]{:S(2)}) async-start(bf16[32,8,896]{2,1,0:T(8,128)(2,1)} %shard_map.148), calls=%async_computation.2 | async-start | bytes 917504 | tf_op jit(solution)/shard_map/all_to_all | solution.py:376
  46.0 1.7 %collective-permute-start.1 = (bf16[3,64,512]{2,1,0:T(8,128)(2,1)S(1)}, bf16[3,64,512]{2,1,0:T(8,128)(2,1)S(1)}, u32[]{:S(2)}, u32[]{:S(2)}) collective-permute-start(bf16[3,64,512]{2,1,0:T(8,128)(2,1)S(1)} %get-tuple-element.24), channel_id=1, source_target_pairs={{0,2},{1,3},{2,0},{3,1},{4,6},{5,7},{6,4},{7,5},{8,10},{9,11},{10,... | collective-permute-start | bytes 589832 | tf_op jit(solution)/shard_map/ppermute | solution.py:273
  47.7 1.5 %collective-permute-start.2 = (bf16[3,64,512]{2,1,0:T(8,128)(2,1)S(1)}, bf16[3,64,512]{2,1,0:T(8,128)(2,1)S(1)}, u32[]{:S(2)}, u32[]{:S(2)}) collective-permute-start(bf16[3,64,512]{2,1,0:T(8,128)(2,1)S(1)} %get-tuple-element.25), channel_id=1, source_target_pairs={{0,4},{1,5},{2,6},{3,7},{4,0},{5,1},{6,2},{7,3},{8,12},{9,13},{10,... | collective-permute-start | bytes 589832 | tf_op jit(solution)/shard_map/ppermute | solution.py:273
  49.6 8.4 %collective-permute-done.1.refs_1_ = bf16[3,64,512]{2,1,0:T(8,128)(2,1)S(1)} collective-permute-done((bf16[3,64,512]{2,1,0:T(8,128)(2,1)S(1)}, bf16[3,64,512]{2,1,0:T(8,128)(2,1)S(1)}, u32[]{:S(2)}, u32[]{:S(2)}) %collective-permute-start.1) | collective-permute-done | bytes 196640 | tf_op jit(solution)/shard_map/ppermute | solution.py:273
  58.2 4.8 %collective-permute-done.3.refs_3_ = bf16[3,64,512]{2,1,0:T(8,128)(2,1)S(1)} collective-permute-done((bf16[3,64,512]{2,1,0:T(8,128)(2,1)S(1)}, bf16[3,64,512]{2,1,0:T(8,128)(2,1)S(1)}, u32[]{:S(2)}, u32[]{:S(2)}) %collective-permute-start.3) | collective-permute-done | bytes 196640 | tf_op jit(solution)/shard_map/ppermute | solution.py:273
  63.1 1.6 %collective-permute-start.4 = (bf16[3,16,512]{2,1,0:T(8,128)(2,1)S(1)}, bf16[3,16,512]{2,1,0:T(8,128)(2,1)S(1)}, u32[]{:S(2)}, u32[]{:S(2)}) collective-permute-start(bf16[3,16,512]{2,1,0:T(8,128)(2,1)S(1)} %get-tuple-element.28), channel_id=1, source_target_pairs={{0,8},{1,9},{2,10},{3,11},{4,12},{5,13},{6,14},{7,15},{8,0},{9,1},... | collective-permute-start | bytes 147464 | tf_op jit(solution)/shard_map/ppermute | solution.py:273
  64.7 2.4 %collective-permute-start.5 = (bf16[3,16,512]{2,1,0:T(8,128)(2,1)S(1)}, bf16[3,16,512]{2,1,0:T(8,128)(2,1)S(1)}, u32[]{:S(2)}, u32[]{:S(2)}) collective-permute-start(bf16[3,16,512]{2,1,0:T(8,128)(2,1)S(1)} %get-tuple-element.29), channel_id=1, source_target_pairs={{0,16},{1,17},{2,18},{3,19},{4,20},{5,21},{6,22},{7,23},{8,24},{9,... | collective-permute-start | bytes 147464 | tf_op jit(solution)/shard_map/ppermute | solution.py:273
  67.6 2.8 %collective-permute-done.5.refs_2_ = bf16[3,16,512]{2,1,0:T(8,128)(2,1)S(1)} collective-permute-done((bf16[3,16,512]{2,1,0:T(8,128)(2,1)S(1)}, bf16[3,16,512]{2,1,0:T(8,128)(2,1)S(1)}, u32[]{:S(2)}, u32[]{:S(2)}) %collective-permute-start.5) | collective-permute-done | bytes 49184 | tf_op jit(solution)/shard_map/ppermute | solution.py:273
  70.3 2.7 %collective-permute-done.6.refs_3_ = bf16[3,16,512]{2,1,0:T(8,128)(2,1)S(1)} collective-permute-done((bf16[3,16,512]{2,1,0:T(8,128)(2,1)S(1)}, bf16[3,16,512]{2,1,0:T(8,128)(2,1)S(1)}, u32[]{:S(2)}, u32[]{:S(2)}) %collective-permute-start.6) | collective-permute-done | bytes 49184 | tf_op jit(solution)/shard_map/ppermute | solution.py:273
  73.8 3.7 %collective-permute-start.7 = (bf16[3,16,512]{2,1,0:T(8,128)(2,1)S(1)}, bf16[3,16,512]{2,1,0:T(8,128)(2,1)S(1)}, u32[]{:S(2)}, u32[]{:S(2)}) collective-permute-start(bf16[3,16,512]{2,1,0:T(8,128)(2,1)S(1)} %shard_map.150.refs_0_), channel_id=1, source_target_pairs={{0,8},{1,9},{2,10},{3,11},{4,12},{5,13},{6,14},{7,15},{8,0},{9,1},... | collective-permute-start | bytes 147464 | tf_op jit(solution)/shard_map/ppermute | solution.py:273
  77.6 1.6 %collective-permute-done.9.refs_3_ = bf16[3,16,512]{2,1,0:T(8,128)(2,1)S(1)} collective-permute-done((bf16[3,16,512]{2,1,0:T(8,128)(2,1)S(1)}, bf16[3,16,512]{2,1,0:T(8,128)(2,1)S(1)}, u32[]{:S(2)}, u32[]{:S(2)}) %collective-permute-start.9) | collective-permute-done | bytes 49184 | tf_op jit(solution)/shard_map/ppermute | solution.py:273
  80.6 1.3 %collective-permute-start.11 = (bf16[3,64,512]{2,1,0:T(8,128)(2,1)S(1)}, bf16[3,64,512]{2,1,0:T(8,128)(2,1)S(1)}, u32[]{:S(2)}, u32[]{:S(2)}) collective-permute-start(bf16[3,64,512]{2,1,0:T(8,128)(2,1)S(1)} %shard_map.151.after_ref.refs_0_), channel_id=1, source_target_pairs={{0,4},{1,5},{2,6},{3,7},{4,0},{5,1},{6,2},{7,3},{8,12},{9,13},{10,... | collective-permute-start | bytes 589832 | tf_op jit(solution)/shard_map/ppermute | solution.py:273
  81.9 1.4 %collective-permute-start.10 = (bf16[3,64,512]{2,1,0:T(8,128)(2,1)S(1)}, bf16[3,64,512]{2,1,0:T(8,128)(2,1)S(1)}, u32[]{:S(2)}, u32[]{:S(2)}) collective-permute-start(bf16[3,64,512]{2,1,0:T(8,128)(2,1)S(1)} %shard_map.151.after_ref.refs_0_), channel_id=1, source_target_pairs={{0,2},{1,3},{2,0},{3,1},{4,6},{5,7},{6,4},{7,5},{8,10},{9,11},{10,... | collective-permute-start | bytes 589832 | tf_op jit(solution)/shard_map/ppermute | solution.py:273
  83.4 3.7 %collective-permute-done.12.refs_3_ = bf16[3,64,512]{2,1,0:T(8,128)(2,1)S(1)} collective-permute-done((bf16[3,64,512]{2,1,0:T(8,128)(2,1)S(1)}, bf16[3,64,512]{2,1,0:T(8,128)(2,1)S(1)}, u32[]{:S(2)}, u32[]{:S(2)}) %collective-permute-start.12) | collective-permute-done | bytes 196640 | tf_op jit(solution)/shard_map/ppermute | solution.py:273
  87.1 1.4 %collective-permute-done.11.refs_2_ = bf16[3,64,512]{2,1,0:T(8,128)(2,1)S(1)} collective-permute-done((bf16[3,64,512]{2,1,0:T(8,128)(2,1)S(1)}, bf16[3,64,512]{2,1,0:T(8,128)(2,1)S(1)}, u32[]{:S(2)}, u32[]{:S(2)}) %collective-permute-start.11) | collective-permute-done | bytes 196640 | tf_op jit(solution)/shard_map/ppermute | solution.py:273
  88.9 2.1 %shard_map.153 = f32[320,512]{1,0:T(8,128)} custom-call(s32[32,12]{1,0:T(8,128)S(1)} %reshape.26.rows_ref, bf16[384,512]{1,0:T(8,128)(2,1)S(1)} %get-tuple-element.20.pre_ref, bf16[512,512]{1,0:T(8,128)(2,1)S(1)} %copy-done.2, f32[3,64,512]{2,1,0:T(8,128)S(1)} %get-tuple-element.23.after_ref.refs_0_), custom_call_target="tpu_custom_call" | custom-call | flops 671088640 | tf_op jit(solution)/shard_map/pallas_call | solution.py:44
  91.1 1.9 %shard_map.154 = (f32[512,512]{1,0:T(8,128)}, f32[512,512]{1,0:T(8,128)}, f32[512,512]{1,0:T(8,128)}) custom-call(bf16[3,64,512]{2,1,0:T(8,128)(2,1)S(1)} %shard_map.151.after_ref.refs_0_, bf16[3,64,512]{2,1,0:T(8,128)(2,1)S(1)} %collective-permute-done.10.refs_1_, bf16[3,64,512]{2,1,0:T(8,128)(2,1)S(1)} %collective-permute-done.11.refs_2_, ...), custom_call_target="tpu_custom_call" | custom-call | tf_op jit(solution)/shard_map/pallas_call | solution.py:44
  93.6 6.4 %shard_map.152 = f32[4096,512]{1,0:T(8,128)} custom-call(s32[32,12]{1,0:T(8,128)S(1)} %bitcast.6, bf16[32,8,896]{2,1,0:T(8,128)(2,1)S(1)} %all-to-all-done.2.came_ref, bf16[3,64,512]{2,1,0:T(8,128)(2,1)S(1)} %shard_map.151.after_ref.refs_0_), custom_call_target="tpu_custom_call" | custom-call | flops 1610612736 | bytes 8388608 | tf_op jit(solution)/shard_map/pallas_call | solution.py:389
  (41 shorter events, 6.9 us)
Async XLA Ops:
  0.6 22.1 %copy-start.5 = (s32[1,32]{1,0:T(1,128)S(1)}, s32[1,32]{1,0:T(1,128)}, u32[]{:S(2)}) copy-start(s32[1,32]{1,0:T(1,128)} %param.15) | copy-start | bytes 388
  0.7 35.2 %copy-start.2 = (bf16[512,512]{1,0:T(8,128)(2,1)S(1)}, bf16[512,512]{1,0:T(8,128)(2,1)}, u32[]{:S(2)}) copy-start(bf16[512,512]{1,0:T(8,128)(2,1)} %w1_ref.3) | copy-start | bytes 1572868
  0.7 35.2 %copy-start = (bf16[512,512]{1,0:T(8,128)(2,1)S(1)}, bf16[512,512]{1,0:T(8,128)(2,1)}, u32[]{:S(2)}) copy-start(bf16[512,512]{1,0:T(8,128)(2,1)} %w1_ref.2) | copy-start | bytes 1572868
  0.7 35.2 %copy-start.1 = (bf16[512,512]{1,0:T(8,128)(2,1)S(1)}, bf16[512,512]{1,0:T(8,128)(2,1)}, u32[]{:S(2)}) copy-start(bf16[512,512]{1,0:T(8,128)(2,1)} %w2_ref.1) | copy-start | bytes 1572868
  0.7 35.2 %copy-start.3 = (f32[512]{0:T(512)S(1)}, f32[512]{0:T(512)}, u32[]{:S(2)}) copy-start(f32[512]{0:T(512)} %param.18) | copy-start | bytes 6148
  20.0 15.9 %all-to-all-start.1 = ((bf16[32,8,768]{2,1,0:T(8,128)(2,1)}), bf16[32,8,768]{2,1,0:T(8,128)(2,1)S(1)}, u32[]{:S(2)}, u32[]{:S(2)}) async-start(bf16[32,8,768]{2,1,0:T(8,128)(2,1)} %shard_map.145), calls=%async_computation.1 | async-start | bytes 786432 | tf_op jit(solution)/shard_map/all_to_all | solution.py:340
  39.7 2.4 %collective-permute-start = (bf16[3,256,512]{2,1,0:T(8,128)(2,1)S(1)}, bf16[3,256,512]{2,1,0:T(8,128)(2,1)S(1)}, u32[]{:S(2)}, u32[]{:S(2)}) collective-permute-start(bf16[3,256,512]{2,1,0:T(8,128)(2,1)S(1)} %get-tuple-element.22), channel_id=1, source_target_pairs={{0,1},{1,0},{2,3},{3,2},{4,5},{5,4},{6,7},{7,6},{8,9},{9,8},{10,11... | collective-permute-start | bytes 2359304 | tf_op jit(solution)/shard_map/ppermute | solution.py:273
  43.4 49.5 %all-to-all-start.2 = ((bf16[32,8,896]{2,1,0:T(8,128)(2,1)}), bf16[32,8,896]{2,1,0:T(8,128)(2,1)S(1)}, u32[]{:S(2)}, u32[]{:S(2)}) async-start(bf16[32,8,896]{2,1,0:T(8,128)(2,1)} %shard_map.148), calls=%async_computation.2 | async-start | bytes 917504 | tf_op jit(solution)/shard_map/all_to_all | solution.py:376
  46.0 12.0 %collective-permute-start.1 = (bf16[3,64,512]{2,1,0:T(8,128)(2,1)S(1)}, bf16[3,64,512]{2,1,0:T(8,128)(2,1)S(1)}, u32[]{:S(2)}, u32[]{:S(2)}) collective-permute-start(bf16[3,64,512]{2,1,0:T(8,128)(2,1)S(1)} %get-tuple-element.24), channel_id=1, source_target_pairs={{0,2},{1,3},{2,0},{3,1},{4,6},{5,7},{6,4},{7,5},{8,10},{9,11},{10,... | collective-permute-start | bytes 589832 | tf_op jit(solution)/shard_map/ppermute | solution.py:273
  47.7 10.5 %collective-permute-start.2 = (bf16[3,64,512]{2,1,0:T(8,128)(2,1)S(1)}, bf16[3,64,512]{2,1,0:T(8,128)(2,1)S(1)}, u32[]{:S(2)}, u32[]{:S(2)}) collective-permute-start(bf16[3,64,512]{2,1,0:T(8,128)(2,1)S(1)} %get-tuple-element.25), channel_id=1, source_target_pairs={{0,4},{1,5},{2,6},{3,7},{4,0},{5,1},{6,2},{7,3},{8,12},{9,13},{10,... | collective-permute-start | bytes 589832 | tf_op jit(solution)/shard_map/ppermute | solution.py:273
  49.2 13.8 %collective-permute-start.3 = (bf16[3,64,512]{2,1,0:T(8,128)(2,1)S(1)}, bf16[3,64,512]{2,1,0:T(8,128)(2,1)S(1)}, u32[]{:S(2)}, u32[]{:S(2)}) collective-permute-start(bf16[3,64,512]{2,1,0:T(8,128)(2,1)S(1)} %get-tuple-element.26), channel_id=1, source_target_pairs={{0,6},{1,7},{2,4},{3,5},{4,2},{5,3},{6,0},{7,1},{8,14},{9,15},{10,... | collective-permute-start | bytes 589832 | tf_op jit(solution)/shard_map/ppermute | solution.py:273
  63.1 4.5 %collective-permute-start.4 = (bf16[3,16,512]{2,1,0:T(8,128)(2,1)S(1)}, bf16[3,16,512]{2,1,0:T(8,128)(2,1)S(1)}, u32[]{:S(2)}, u32[]{:S(2)}) collective-permute-start(bf16[3,16,512]{2,1,0:T(8,128)(2,1)S(1)} %get-tuple-element.28), channel_id=1, source_target_pairs={{0,8},{1,9},{2,10},{3,11},{4,12},{5,13},{6,14},{7,15},{8,0},{9,1},... | collective-permute-start | bytes 147464 | tf_op jit(solution)/shard_map/ppermute | solution.py:273
  64.7 5.6 %collective-permute-start.5 = (bf16[3,16,512]{2,1,0:T(8,128)(2,1)S(1)}, bf16[3,16,512]{2,1,0:T(8,128)(2,1)S(1)}, u32[]{:S(2)}, u32[]{:S(2)}) collective-permute-start(bf16[3,16,512]{2,1,0:T(8,128)(2,1)S(1)} %get-tuple-element.29), channel_id=1, source_target_pairs={{0,16},{1,17},{2,18},{3,19},{4,20},{5,21},{6,22},{7,23},{8,24},{9,... | collective-permute-start | bytes 147464 | tf_op jit(solution)/shard_map/ppermute | solution.py:273
  67.1 5.9 %collective-permute-start.6 = (bf16[3,16,512]{2,1,0:T(8,128)(2,1)S(1)}, bf16[3,16,512]{2,1,0:T(8,128)(2,1)S(1)}, u32[]{:S(2)}, u32[]{:S(2)}) collective-permute-start(bf16[3,16,512]{2,1,0:T(8,128)(2,1)S(1)} %get-tuple-element.30), channel_id=1, source_target_pairs={{0,24},{1,25},{2,26},{3,27},{4,28},{5,29},{6,30},{7,31},{8,16},{9,... | collective-permute-start | bytes 147464 | tf_op jit(solution)/shard_map/ppermute | solution.py:273
  73.1 6.1 %collective-permute-start.9 = (bf16[3,16,512]{2,1,0:T(8,128)(2,1)S(1)}, bf16[3,16,512]{2,1,0:T(8,128)(2,1)S(1)}, u32[]{:S(2)}, u32[]{:S(2)}) collective-permute-start(bf16[3,16,512]{2,1,0:T(8,128)(2,1)S(1)} %shard_map.150.refs_0_), channel_id=1, source_target_pairs={{0,24},{1,25},{2,26},{3,27},{4,28},{5,29},{6,30},{7,31},{8,16},{9,... | collective-permute-start | bytes 147464 | tf_op jit(solution)/shard_map/ppermute | solution.py:273
  73.7 6.0 %collective-permute-start.8 = (bf16[3,16,512]{2,1,0:T(8,128)(2,1)S(1)}, bf16[3,16,512]{2,1,0:T(8,128)(2,1)S(1)}, u32[]{:S(2)}, u32[]{:S(2)}) collective-permute-start(bf16[3,16,512]{2,1,0:T(8,128)(2,1)S(1)} %shard_map.150.refs_0_), channel_id=1, source_target_pairs={{0,16},{1,17},{2,18},{3,19},{4,20},{5,21},{6,22},{7,23},{8,24},{9,... | collective-permute-start | bytes 147464 | tf_op jit(solution)/shard_map/ppermute | solution.py:273
  73.8 6.0 %collective-permute-start.7 = (bf16[3,16,512]{2,1,0:T(8,128)(2,1)S(1)}, bf16[3,16,512]{2,1,0:T(8,128)(2,1)S(1)}, u32[]{:S(2)}, u32[]{:S(2)}) collective-permute-start(bf16[3,16,512]{2,1,0:T(8,128)(2,1)S(1)} %shard_map.150.refs_0_), channel_id=1, source_target_pairs={{0,8},{1,9},{2,10},{3,11},{4,12},{5,13},{6,14},{7,15},{8,0},{9,1},... | collective-permute-start | bytes 147464 | tf_op jit(solution)/shard_map/ppermute | solution.py:273
  79.8 7.2 %collective-permute-start.12 = (bf16[3,64,512]{2,1,0:T(8,128)(2,1)S(1)}, bf16[3,64,512]{2,1,0:T(8,128)(2,1)S(1)}, u32[]{:S(2)}, u32[]{:S(2)}) collective-permute-start(bf16[3,64,512]{2,1,0:T(8,128)(2,1)S(1)} %shard_map.151.after_ref.refs_0_), channel_id=1, source_target_pairs={{0,6},{1,7},{2,4},{3,5},{4,2},{5,3},{6,0},{7,1},{8,14},{9,15},{10,... | collective-permute-start | bytes 589832 | tf_op jit(solution)/shard_map/ppermute | solution.py:273
  80.6 7.8 %collective-permute-start.11 = (bf16[3,64,512]{2,1,0:T(8,128)(2,1)S(1)}, bf16[3,64,512]{2,1,0:T(8,128)(2,1)S(1)}, u32[]{:S(2)}, u32[]{:S(2)}) collective-permute-start(bf16[3,64,512]{2,1,0:T(8,128)(2,1)S(1)} %shard_map.151.after_ref.refs_0_), channel_id=1, source_target_pairs={{0,4},{1,5},{2,6},{3,7},{4,0},{5,1},{6,2},{7,3},{8,12},{9,13},{10,... | collective-permute-start | bytes 589832 | tf_op jit(solution)/shard_map/ppermute | solution.py:273
  81.9 6.5 %collective-permute-start.10 = (bf16[3,64,512]{2,1,0:T(8,128)(2,1)S(1)}, bf16[3,64,512]{2,1,0:T(8,128)(2,1)S(1)}, u32[]{:S(2)}, u32[]{:S(2)}) collective-permute-start(bf16[3,64,512]{2,1,0:T(8,128)(2,1)S(1)} %shard_map.151.after_ref.refs_0_), channel_id=1, source_target_pairs={{0,2},{1,3},{2,0},{3,1},{4,6},{5,7},{6,4},{7,5},{8,10},{9,11},{10,... | collective-permute-start | bytes 589832 | tf_op jit(solution)/shard_map/ppermute | solution.py:273
  83.4 7.7 %collective-permute-start.13 = (bf16[3,64,512]{2,1,0:T(8,128)(2,1)S(1)}, bf16[3,64,512]{2,1,0:T(8,128)(2,1)S(1)}, u32[]{:S(2)}, u32[]{:S(2)}) collective-permute-start(bf16[3,64,512]{2,1,0:T(8,128)(2,1)S(1)} %shard_map.151.after_ref.refs_0_), channel_id=1, source_target_pairs={{0,1},{1,0},{2,3},{3,2},{4,5},{5,4},{6,7},{7,6},{8,9},{9,8},{10,11... | collective-permute-start | bytes 589832 | tf_op jit(solution)/shard_map/ppermute | solution.py:273
  87.0 4.0 %collective-permute-start.16 = (bf16[3,64,512]{2,1,0:T(8,128)(2,1)S(1)}, bf16[3,64,512]{2,1,0:T(8,128)(2,1)S(1)}, u32[]{:S(2)}, u32[]{:S(2)}) collective-permute-start(bf16[3,64,512]{2,1,0:T(8,128)(2,1)S(1)} %collective-permute-done.12.refs_3_), channel_id=1, source_target_pairs={{0,1},{1,0},{2,3},{3,2},{4,5},{5,4},{6,7},{7,6},{8,9},{9,8},{10,11... | collective-permute-start | bytes 589832 | tf_op jit(solution)/shard_map/ppermute | solution.py:273
  88.4 2.6 %collective-permute-start.15 = (bf16[3,64,512]{2,1,0:T(8,128)(2,1)S(1)}, bf16[3,64,512]{2,1,0:T(8,128)(2,1)S(1)}, u32[]{:S(2)}, u32[]{:S(2)}) collective-permute-start(bf16[3,64,512]{2,1,0:T(8,128)(2,1)S(1)} %collective-permute-done.11.refs_2_), channel_id=1, source_target_pairs={{0,1},{1,0},{2,3},{3,2},{4,5},{5,4},{6,7},{7,6},{8,9},{9,8},{10,11... | collective-permute-start | bytes 589832 | tf_op jit(solution)/shard_map/ppermute | solution.py:273
  88.4 2.6 %collective-permute-start.14 = (bf16[3,64,512]{2,1,0:T(8,128)(2,1)S(1)}, bf16[3,64,512]{2,1,0:T(8,128)(2,1)S(1)}, u32[]{:S(2)}, u32[]{:S(2)}) collective-permute-start(bf16[3,64,512]{2,1,0:T(8,128)(2,1)S(1)} %collective-permute-done.10.refs_1_), channel_id=1, source_target_pairs={{0,1},{1,0},{2,3},{3,2},{4,5},{5,4},{6,7},{7,6},{8,9},{9,8},{10,11... | collective-permute-start | bytes 589832 | tf_op jit(solution)/shard_map/ppermute | solution.py:273
  (1 other events, 22.0 us)

commit v3 on v2

--- a/solution.py
+++ b/solution.py
@@ -10,12 +10,14 @@
 
 
 SUB = 8
+BLOCK = 512
+RING = 4
 HALF = SUB // 2
 F32 = jnp.float32
 BF16 = jnp.bfloat16
 WHOLE = pl.BlockSpec(memory_space=pltpu.VMEM)
 FAR = pl.BlockSpec(memory_space=pltpu.HBM)
-GRANT = pltpu.CompilerParams(vmem_limit_bytes=30 << 20)
+GRANT = pltpu.CompilerParams(vmem_limit_bytes=32 << 20)
 
 
 def dot(left, right, dims=((1,), (0,))):
@@ -34,14 +36,22 @@
     make = jax.ShapeDtypeStruct if leaves else pltpu.VMEM
     built = pl.pallas_call(
         kernel,
-        **({} if specs is None else {"in_specs": specs}),
+        **({} if specs is None else {"in_specs": [spec or WHOLE for spec in specs]}),
         out_shape=[make(shape, dtype) for shape, dtype in outs],
         scratch_shapes=list(scratch),
         compiler_params=GRANT,
         cost_estimate=pl.CostEstimate(flops=flops, transcendentals=0, bytes_accessed=0),
     )
-    places = [near] * 99 if specs is None else [far if spec is FAR else near for spec in specs]
-    return lambda *values: built(*(place(value) for place, value in zip(places, values)))
+
+    def run(*values):
+        places = [WHOLE] * len(values) if specs is None else specs
+        moved = [
+            value if spec is None else far(value) if spec is FAR else near(value)
+            for spec, value in zip(places, values)
+        ]
+        return built(*moved)
+
+    return run
 
 
 def column(index):
@@ -117,49 +127,62 @@
     out_ref[:, :, width:] = tail.astype(BF16)
 
 
+def mesh_kernel(
+    rows_ref, live_ref, latent_ref, cot_ref, w1_ref, w2_ref, bias_ref, in_ref, grad_ref, base_ref, hid_ref
+):
+    nodes = latent_ref.shape[0]
+    mesh_in = dot(pick(column(rows_ref[...]), 0, nodes), latent_ref[...]).astype(BF16)
+    out_grad = dot(pick(column(live_ref[...]), 0, nodes), cot_ref[...]).astype(BF16)
+    in_ref[...] = mesh_in
+    grad_ref[...] = out_grad
+    base_ref[...] = dot(mesh_in, w1_ref[...]) + bias_ref[...]
+    hid_ref[...] = dot(out_grad, w2_ref[...], ((1,), (1,)))
+
+
 def edge_kernel(
     got_ref,
-    rows_ref,
-    live_ref,
-    latent_ref,
-    cot_ref,
-    w1m_ref,
-    w2_ref,
-    bias_ref,
-    w1g_ref,
+    base_hbm,
+    hid_hbm,
+    mesh_hbm,
+    grad_hbm,
+    w1_ref,
     sent_ref,
     kept_ref,
     pre_ref,
     full_ref,
-    latent_vmem,
-    cot_vmem,
+    base_ref,
+    hid_ref,
+    mesh_ref,
+    grad_ref,
     sems,
 ):
-    nodes, width = latent_ref.shape
-    load_latent = pltpu.make_async_copy(latent_ref, latent_vmem, sems.at[0])
-    load_cot = pltpu.make_async_copy(cot_ref, cot_vmem, sems.at[1])
-    load_latent.start()
-    load_cot.start()
+    loads = [
+        pltpu.make_async_copy(source, held, sems.at[which])
+        for which, (source, held) in enumerate(
+            ((base_hbm, base_ref), (hid_hbm, hid_ref), (mesh_hbm, mesh_ref), (grad_hbm, grad_ref))
+        )
+    ]
+    for load in loads:
+        load.start()
+    width = mesh_ref.shape[1]
     half = sent_ref.shape[1]
     core = lax.rem(lax.axis_index("patch"), 2)
     grid_in = unpack(got_ref[...].astype(F32), width).astype(BF16)
-    grid_proj = dot(grid_in, w1g_ref[...]).astype(BF16).astype(F32)
-    picked = pick(column(rows_ref[...]), 0, nodes)
-    live = pick(column(live_ref[...]), 0, nodes)
-    load_latent.wait()
-    mesh_in = dot(picked, latent_vmem[...]).astype(BF16)
-    load_cot.wait()
-    out_grad = dot(live, cot_vmem[...]).astype(BF16)
-    before = grid_proj + dot(mesh_in, w1m_ref[...]) + bias_ref[...]
+    grid_proj = dot(grid_in, w1_ref[...]).astype(BF16).astype(F32)
+    loads[0].wait()
+    before = grid_proj + base_ref[...]
     logistic = jax.nn.sigmoid(before)
     hidden = (before * logistic).astype(BF16)
     derivative = logistic * (1.0 + before * (1.0 - logistic))
-    pre = (dot(out_grad, w2_ref[...], ((1,), (1,))) * derivative).astype(BF16)
+    loads[1].wait()
+    pre = (hid_ref[...] * derivative).astype(BF16)
     pre_ref[...] = pre
     across = ((0,), (0,))
     full_ref[0] = dot(grid_in, pre, across)
-    full_ref[1] = dot(mesh_in, pre, across)
-    full_ref[2] = dot(hidden, out_grad, across)
+    loads[2].wait()
+    full_ref[1] = dot(mesh_ref[...], pre, across)
+    loads[3].wait()
+    full_ref[2] = dot(hidden, grad_ref[...], across)
     away = pl.multiple_of((1 - core) * half, half)
     home = pl.multiple_of(core * half, half)
     for which in range(3):
@@ -167,7 +190,7 @@
         kept_ref[which] = full_ref[which, pl.ds(home, half), :]
 
 
-def return_kernel(pre_ref, w1_ref, after_ref, out_ref):
+def return_kernel(pre_ref, w1_ref, out_ref):
     members = out_ref.shape[0]
     width = pre_ref.shape[1]
     pre = pre_ref[...]
@@ -188,28 +211,33 @@
     )
 
 
-def scatter_kernel(index_ref, came_ref, after_ref, out_ref, rows_ref, flat_ref):
-    step = pl.program_id(0)
-    size, width = out_ref.shape
-
-    @pl.when(step == 0)
-    def _():
-        flat_ref[...] = jnp.broadcast_to(lanes(index_ref[...]), flat_ref.shape)
-        rows_ref[...] = unpack(came_ref[...].astype(F32), width).astype(BF16)
-
-    at = lax.broadcasted_iota(jnp.int32, (size, rows_ref.shape[0]), 0) + step * size
-    chosen = jnp.where(at == flat_ref[:1], 1.0, 0.0).astype(BF16)
-    out_ref[...] = dot(chosen, rows_ref[...])
-
-
-def bias_kernel(scale, came_ref, out_ref):
-    width = out_ref.shape[1]
+def scatter_kernel(
+    scale, index_ref, came_ref, after_ref, out_ref, bias_ref, rows_ref, held_ref, sems
+):
+    ring, size, width = held_ref.shape
+    rows_ref[...] = unpack(came_ref[...].astype(F32), width).astype(BF16)
+    flat = lanes(index_ref[...])
+    copies = []
+    for step in range(out_ref.shape[0] // size):
+        slot = step % ring
+        if step >= ring:
+            copies[step - ring].wait()
+        at = lax.broadcasted_iota(jnp.int32, (size, rows_ref.shape[0]), 0) + step * size
+        chosen = jnp.where(at == flat, 1.0, 0.0).astype(BF16)
+        held_ref[slot] = dot(chosen, rows_ref[...])
+        copy = pltpu.make_async_copy(
+            held_ref.at[slot], out_ref.at[pl.ds(step * size, size), :], sems.at[slot]
+        )
+        copy.start()
+        copies.append(copy)
     tile = jnp.sum(came_ref[:, :, width + width // 2 :].astype(F32), axis=0)
     for part in range(width // 128):
         low = part + width // 128
-        out_ref[:, part * 128 : part * 128 + 128] = (
+        bias_ref[:, part * 128 : part * 128 + 128] = (
             tile[part : part + 1] + tile[low : low + 1]
         ) * scale
+    for copy in copies[-ring:]:
+        copy.wait()
 
 
 def node_kernel(rows_ref, pre_ref, w1_ref, after_ref, out_ref):
@@ -274,16 +302,25 @@
 
 
 def final_kernel(scale, stride, size, *refs):
-    pieces, outputs = refs[: 2 * size], refs[2 * size :]
+    pieces = refs[: 2 * size]
+    *outputs, held_ref, sems = refs[2 * size :]
     core = lax.rem(lax.axis_index("patch"), 2)
     here = place(stride, size)
     cut = pieces[0].shape[1]
-    for side in range(2):
-        base = (core if side == 0 else 1 - core) * (cut * size)
-        for k in range(size):
-            start = pl.multiple_of(base + (here ^ k) * cut, cut)
-            for which, out_ref in enumerate(outputs):
-                out_ref[pl.ds(start, cut), :] = pieces[side * size + k][which].astype(F32) * scale
+    copies = []
+    for which, out_ref in enumerate(outputs):
+        for side in range(2):
+            base = (core if side == 0 else 1 - core) * (cut * size)
+            for k in range(size):
+                start = pl.multiple_of(base + (here ^ k) * cut, cut)
+                held_ref[which, pl.ds(start, cut), :] = (
+                    pieces[side * size + k][which].astype(F32) * scale
+                )
+        copy = pltpu.make_async_copy(held_ref.at[which], out_ref, sems.at[which])
+        copy.start()
+        copies.append(copy)
+    for copy in copies:
+        copy.wait()
 
 
 def body(
@@ -340,28 +377,24 @@
     got = swap(found)
     flat = (slots, width)
     halves = (3, width // 2, width)
+    mesh_side = [(flat, BF16), (flat, BF16), (flat, F32), (flat, F32)]
+    mesh_in, out_grad, base, hid = call(
+        mesh_kernel, mesh_side, flops=8 * slots * width**2, leaves=True, specs=[WHOLE] * 2 + [None] * 5
+    )(rows2d, live2d, mesh_latent, mesh_cotangent, w1_mesh, w2, bias_one.reshape(1, width))
     sent, kept, pre = call(
         edge_kernel,
         [(halves, BF16), (halves, F32), (flat, BF16)],
         [
             pltpu.VMEM((3, width, width), F32),
-            pltpu.VMEM((nodes, width), BF16),
-            pltpu.VMEM((nodes, width), BF16),
-            pltpu.SemaphoreType.DMA((2,)),
+            pltpu.VMEM(flat, F32),
+            pltpu.VMEM(flat, F32),
+            pltpu.VMEM(flat, BF16),
+            pltpu.VMEM(flat, BF16),
+            pltpu.SemaphoreType.DMA((4,)),
         ],
-        flops=14 * slots * width**2,
-        specs=[WHOLE, WHOLE, WHOLE, FAR, FAR, WHOLE, WHOLE, WHOLE, WHOLE],
-    )(
-        got,
-        rows2d,
-        live2d,
-        mesh_latent,
-        mesh_cotangent,
-        w1_mesh,
-        w2,
-        bias_one.reshape(1, width),
-        w1_grid,
-    )
+        flops=8 * slots * width**2,
+        specs=[WHOLE, FAR, FAR, FAR, FAR, WHOLE],
+    )(got, base, hid, mesh_in, out_grad, w1_grid)
 
     came = [send(sent, 1, members)]
     own = kept
@@ -372,7 +405,7 @@
         after = own if after is None else after
 
     wide = (members, SUB, 2 * width - width // 2 + 128)
-    leaving = call(return_kernel, [(wide, BF16)], flops=2 * slots * width**2)(pre, w1_grid, after)[0]
+    leaving = call(return_kernel, [(wide, BF16)], flops=2 * slots * width**2)(pre, w1_grid)[0]
     returned = swap(leaving)
     mesh_grad = call(
         node_kernel, [((nodes, width), F32)], flops=8 * nodes * width**2, leaves=True
@@ -385,26 +418,34 @@
         if position > 0:
             pieces = [join(pieces, stride)]
     stride, size = steps[0]
-    block = min(512, points)
-    grid_grad = pl.pallas_call(
-        scatter_kernel,
-        out_shape=jax.ShapeDtypeStruct((points, width), F32),
-        grid=(points // block,),
+    block = min(BLOCK, points)
+    ring = min(RING, points // block)
+    grid_grad, bias_grad = pl.pallas_call(
+        functools.partial(scatter_kernel, scale),
+        out_shape=[
+            jax.ShapeDtypeStruct((points, width), F32),
+            jax.ShapeDtypeStruct((1, width), F32),
+        ],
         compiler_params=GRANT,
         in_specs=[WHOLE, WHOLE, WHOLE],
-        out_specs=pl.BlockSpec((block, width), lambda i: (i, 0)),
-        scratch_shapes=[pltpu.VMEM(flat, BF16), pltpu.VMEM((SUB, slots), jnp.int32)],
+        out_specs=[FAR, WHOLE],
+        scratch_shapes=[
+            pltpu.VMEM(flat, BF16),
+            pltpu.VMEM((ring, block, width), F32),
+            pltpu.SemaphoreType.DMA((ring,)),
+        ],
         cost_estimate=pl.CostEstimate(
             flops=2 * slots * points * width, transcendentals=0, bytes_accessed=4 * points * width
         ),
     )(near(wanted), near(returned), near(pieces[0]))
     others = [send(piece, 1, members) for piece in pieces]
-    grads = call(
-        functools.partial(final_kernel, scale, stride, size), [((width, width), F32)] * 3, leaves=True
-    )(*pieces, *others)
-    bias_grad = call(functools.partial(bias_kernel, scale), [((1, width), F32)], leaves=True)(
-        returned
-    )[0]
+    grads = pl.pallas_call(
+        functools.partial(final_kernel, scale, stride, size),
+        out_shape=[jax.ShapeDtypeStruct((width, width), F32)] * 3,
+        out_specs=[FAR] * 3,
+        scratch_shapes=[pltpu.VMEM((3, width, width), F32), pltpu.SemaphoreType.DMA((3,))],
+        compiler_params=GRANT,
+    )(*map(near, (*pieces, *others)))
     return (grid_grad, mesh_grad, *grads, bias_grad.reshape(width))
 
 

time: 100 us -> 99.3 us (level)
  waiting for transfers between devices: 41.5 us -> 33.5 us
  local copies, waits for them, and re-layouts: 1.02 us -> 8 us
    unnamed x12 -> x30, local copies, waits for them, and re-layouts: 0.03 us -> 7.02 us
    all_to_all x1, waiting for transfers between devices: 13.1 us -> 7.44 us  [body(): got = swap(found)]
    ppermute x17, waiting for transfers between devices: 28.5 us -> 26.1 us  [send(): return lax.ppermute(value, 'patch', [(i, i ^ step) for i in range(members)])]
  transfers between devices with their start and end apart: 19 -> 19, of which waited for: 11 -> 10; matrix products, arithmetic and copies ran while one was open for 0% -> 0% of each run, Pallas kernels for 4% -> 10%
where the time goes in v3:
time: 99.3 us; the launch traced here: 98.9 us
  waiting for transfers between devices  33.5 us (34%)
  starting transfers between devices  21.8 us (22%)
  Pallas kernels  20.3 us (20%)
  blocking collectives  14.3 us (14%)
  local copies, waits for them, and re-layouts  8 us (8%)
    ppermute x17, waiting for transfers between devices, send(): return lax.ppermute(value, 'patch', [(i, i ^ step) for i in range(members)])  26.1 us
    ppermute x17, starting transfers between devices, send(): return lax.ppermute(value, 'patch', [(i, i ^ step) for i in range(members)])  16.6 us
    all_to_all x1, blocking collectives, body(): wanted = swap(grid_rows.reshape(members, capacity))  14.3 us
    pallas_call x8, Pallas kernels, run(): return built(*moved)  9.25 us
    all_to_all x1, waiting for transfers between devices, body(): got = swap(found)  7.44 us
    unnamed x30, local copies, waits for them, and re-layouts  7.02 us
    pallas_call x1, Pallas kernels, body(): pl.pallas_call(functools.partial(scatter_kernel, scale), out_shape=[jax.S...  5.09 us
    pallas_call x1, Pallas kernels, body(): pl.pallas_call(gather_kernel, out_shape=pltpu.VMEM(packed, BF16), in_spec...  4.18 us
  transfers between devices with their start and end apart: 19, of which 10 were waited for; matrix products, arithmetic and copies ran while one was open for 0% of the time, Pallas kernels for 10%

profile of v3, /device:TPU:0, one launch (start us, length us, event | category | flops | bytes accessed | tf_op | source)
XLA Modules:
  0.0 98.9 jit_solution(4693343765669206056)
XLA Ops:
  1.6 14.3 %all_to_all.21 = s32[32,1,12]{2,1,0:T(1,128)S(1)} all-to-all(s32[32,1,12]{2,1,0:T(1,128)S(1)} %bitcast.8), channel_id=1, replica_groups=mesh['patch'=32] {'patch'}, dimensions={0} | all-to-all | bytes 3072 | tf_op jit(solution)/shard_map/all_to_all | solution.py:357
  15.9 4.2 %shard_map.145 = bf16[32,8,768]{2,1,0:T(8,128)(2,1)} custom-call(s32[32,12]{1,0:T(8,128)S(1)} %bitcast.5, bf16[4096,512]{1,0:T(8,128)(2,1)} %table_ref.1), custom_call_target="tpu_custom_call" | custom-call | flops 1610612736 | bytes 4194304 | tf_op jit(solution)/shard_map/pallas_call | solution.py:363
  20.1 2.6 %all-to-all-start.1 = ((bf16[32,8,768]{2,1,0:T(8,128)(2,1)}), bf16[32,8,768]{2,1,0:T(8,128)(2,1)S(1)}, u32[]{:S(2)}, u32[]{:S(2)}) async-start(bf16[32,8,768]{2,1,0:T(8,128)(2,1)} %shard_map.145), calls=%async_computation.1 | async-start | bytes 786432 | tf_op jit(solution)/shard_map/all_to_all | solution.py:377
  23.9 1.3 %shard_map.146 = (bf16[384,512]{1,0:T(8,128)(2,1)S(1)}, bf16[384,512]{1,0:T(8,128)(2,1)S(1)}, f32[384,512]{1,0:T(8,128)S(1)}, f32[384,512]{1,0:T(8,128)S(1)}) custom-call(s32[32,12]{1,0:T(8,128)S(1)} %reshape.26.rows_ref, s32[32,12]{1,0:T(8,128)S(1)} %fusion.live_ref, bf16[320,512]{1,0:T(8,128)(2,1)S(1)} %copy-done.10, bf16[320,512]{1,0:T(8,128)(2,1)S(1)} %copy-done.11, ...), custom_call_target="tpu_custom_call" | custom-call | flops 805306368 | tf_op jit(solution)/shard_map/pallas_call | solution.py:52
  28.5 7.4 %all-to-all-done.1.got_ref = bf16[32,8,768]{2,1,0:T(8,128)(2,1)S(1)} async-done(((bf16[32,8,768]{2,1,0:T(8,128)(2,1)}), bf16[32,8,768]{2,1,0:T(8,128)(2,1)S(1)}, u32[]{:S(2)}, u32[]{:S(2)}) %all-to-all-start.1) | async-done | bytes 393248 | tf_op jit(solution)/shard_map/all_to_all | solution.py:377
  36.0 4.3 %shard_map.147 = (bf16[3,256,512]{2,1,0:T(8,128)(2,1)}, f32[3,256,512]{2,1,0:T(8,128)S(1)}, bf16[384,512]{1,0:T(8,128)(2,1)S(1)}) custom-call(bf16[32,8,768]{2,1,0:T(8,128)(2,1)S(1)} %all-to-all-done.1.got_ref, f32[384,512]{1,0:T(8,128)} %copy-done.1, f32[384,512]{1,0:T(8,128)} %copy-done.2, bf16[384,512]{1,0:T(8,128)(2,1)} %copy-done.3, ...), custom_call_target="tpu_custom_call" | custom-call | flops 805306368 | tf_op jit(solution)/shard_map/pallas_call | solution.py:52
  42.3 2.6 %all-to-all-start.2 = ((bf16[32,8,896]{2,1,0:T(8,128)(2,1)}), bf16[32,8,896]{2,1,0:T(8,128)(2,1)S(1)}, u32[]{:S(2)}, u32[]{:S(2)}) async-start(bf16[32,8,896]{2,1,0:T(8,128)(2,1)} %shard_map.148), calls=%async_computation.2 | async-start | bytes 917504 | tf_op jit(solution)/shard_map/all_to_all | solution.py:409
  45.1 1.8 %collective-permute-start.1 = (bf16[3,64,512]{2,1,0:T(8,128)(2,1)S(1)}, bf16[3,64,512]{2,1,0:T(8,128)(2,1)S(1)}, u32[]{:S(2)}, u32[]{:S(2)}) collective-permute-start(bf16[3,64,512]{2,1,0:T(8,128)(2,1)S(1)} %get-tuple-element.34), channel_id=1, source_target_pairs={{0,2},{1,3},{2,0},{3,1},{4,6},{5,7},{6,4},{7,5},{8,10},{9,11},{10,... | collective-permute-start | bytes 589832 | tf_op jit(solution)/shard_map/ppermute | solution.py:301
  46.9 1.5 %collective-permute-start.2 = (bf16[3,64,512]{2,1,0:T(8,128)(2,1)S(1)}, bf16[3,64,512]{2,1,0:T(8,128)(2,1)S(1)}, u32[]{:S(2)}, u32[]{:S(2)}) collective-permute-start(bf16[3,64,512]{2,1,0:T(8,128)(2,1)S(1)} %get-tuple-element.35), channel_id=1, source_target_pairs={{0,4},{1,5},{2,6},{3,7},{4,0},{5,1},{6,2},{7,3},{8,12},{9,13},{10,... | collective-permute-start | bytes 589832 | tf_op jit(solution)/shard_map/ppermute | solution.py:301
  48.6 8.4 %collective-permute-done.1.refs_1_ = bf16[3,64,512]{2,1,0:T(8,128)(2,1)S(1)} collective-permute-done((bf16[3,64,512]{2,1,0:T(8,128)(2,1)S(1)}, bf16[3,64,512]{2,1,0:T(8,128)(2,1)S(1)}, u32[]{:S(2)}, u32[]{:S(2)}) %collective-permute-start.1) | collective-permute-done | bytes 196640 | tf_op jit(solution)/shard_map/ppermute | solution.py:301
  57.1 4.8 %collective-permute-done.3.refs_3_ = bf16[3,64,512]{2,1,0:T(8,128)(2,1)S(1)} collective-permute-done((bf16[3,64,512]{2,1,0:T(8,128)(2,1)S(1)}, bf16[3,64,512]{2,1,0:T(8,128)(2,1)S(1)}, u32[]{:S(2)}, u32[]{:S(2)}) %collective-permute-start.3) | collective-permute-done | bytes 196640 | tf_op jit(solution)/shard_map/ppermute | solution.py:301
  62.0 1.6 %collective-permute-start.4 = (bf16[3,16,512]{2,1,0:T(8,128)(2,1)S(1)}, bf16[3,16,512]{2,1,0:T(8,128)(2,1)S(1)}, u32[]{:S(2)}, u32[]{:S(2)}) collective-permute-start(bf16[3,16,512]{2,1,0:T(8,128)(2,1)S(1)} %get-tuple-element.38), channel_id=1, source_target_pairs={{0,8},{1,9},{2,10},{3,11},{4,12},{5,13},{6,14},{7,15},{8,0},{9,1},... | collective-permute-start | bytes 147464 | tf_op jit(solution)/shard_map/ppermute | solution.py:301
  63.6 2.4 %collective-permute-start.5 = (bf16[3,16,512]{2,1,0:T(8,128)(2,1)S(1)}, bf16[3,16,512]{2,1,0:T(8,128)(2,1)S(1)}, u32[]{:S(2)}, u32[]{:S(2)}) collective-permute-start(bf16[3,16,512]{2,1,0:T(8,128)(2,1)S(1)} %get-tuple-element.39), channel_id=1, source_target_pairs={{0,16},{1,17},{2,18},{3,19},{4,20},{5,21},{6,22},{7,23},{8,24},{9,... | collective-permute-start | bytes 147464 | tf_op jit(solution)/shard_map/ppermute | solution.py:301
  66.5 2.7 %collective-permute-done.5.refs_2_ = bf16[3,16,512]{2,1,0:T(8,128)(2,1)S(1)} collective-permute-done((bf16[3,16,512]{2,1,0:T(8,128)(2,1)S(1)}, bf16[3,16,512]{2,1,0:T(8,128)(2,1)S(1)}, u32[]{:S(2)}, u32[]{:S(2)}) %collective-permute-start.5) | collective-permute-done | bytes 49184 | tf_op jit(solution)/shard_map/ppermute | solution.py:301
  69.2 2.7 %collective-permute-done.6.refs_3_ = bf16[3,16,512]{2,1,0:T(8,128)(2,1)S(1)} collective-permute-done((bf16[3,16,512]{2,1,0:T(8,128)(2,1)S(1)}, bf16[3,16,512]{2,1,0:T(8,128)(2,1)S(1)}, u32[]{:S(2)}, u32[]{:S(2)}) %collective-permute-start.6) | collective-permute-done | bytes 49184 | tf_op jit(solution)/shard_map/ppermute | solution.py:301
  72.7 3.7 %collective-permute-start.7 = (bf16[3,16,512]{2,1,0:T(8,128)(2,1)S(1)}, bf16[3,16,512]{2,1,0:T(8,128)(2,1)S(1)}, u32[]{:S(2)}, u32[]{:S(2)}) collective-permute-start(bf16[3,16,512]{2,1,0:T(8,128)(2,1)S(1)} %shard_map.151.refs_0_), channel_id=1, source_target_pairs={{0,8},{1,9},{2,10},{3,11},{4,12},{5,13},{6,14},{7,15},{8,0},{9,1},... | collective-permute-start | bytes 147464 | tf_op jit(solution)/shard_map/ppermute | solution.py:301
  76.4 1.6 %collective-permute-done.9.refs_3_ = bf16[3,16,512]{2,1,0:T(8,128)(2,1)S(1)} collective-permute-done((bf16[3,16,512]{2,1,0:T(8,128)(2,1)S(1)}, bf16[3,16,512]{2,1,0:T(8,128)(2,1)S(1)}, u32[]{:S(2)}, u32[]{:S(2)}) %collective-permute-start.9) | collective-permute-done | bytes 49184 | tf_op jit(solution)/shard_map/ppermute | solution.py:301
  79.5 1.4 %collective-permute-start.11 = (bf16[3,64,512]{2,1,0:T(8,128)(2,1)S(1)}, bf16[3,64,512]{2,1,0:T(8,128)(2,1)S(1)}, u32[]{:S(2)}, u32[]{:S(2)}) collective-permute-start(bf16[3,64,512]{2,1,0:T(8,128)(2,1)S(1)} %shard_map.152.after_ref.refs_0_), channel_id=1, source_target_pairs={{0,4},{1,5},{2,6},{3,7},{4,0},{5,1},{6,2},{7,3},{8,12},{9,13},{10,... | collective-permute-start | bytes 589832 | tf_op jit(solution)/shard_map/ppermute | solution.py:301
  80.9 1.4 %collective-permute-start.10 = (bf16[3,64,512]{2,1,0:T(8,128)(2,1)S(1)}, bf16[3,64,512]{2,1,0:T(8,128)(2,1)S(1)}, u32[]{:S(2)}, u32[]{:S(2)}) collective-permute-start(bf16[3,64,512]{2,1,0:T(8,128)(2,1)S(1)} %shard_map.152.after_ref.refs_0_), channel_id=1, source_target_pairs={{0,2},{1,3},{2,0},{3,1},{4,6},{5,7},{6,4},{7,5},{8,10},{9,11},{10,... | collective-permute-start | bytes 589832 | tf_op jit(solution)/shard_map/ppermute | solution.py:301
  82.2 3.7 %collective-permute-done.12.refs_3_ = bf16[3,64,512]{2,1,0:T(8,128)(2,1)S(1)} collective-permute-done((bf16[3,64,512]{2,1,0:T(8,128)(2,1)S(1)}, bf16[3,64,512]{2,1,0:T(8,128)(2,1)S(1)}, u32[]{:S(2)}, u32[]{:S(2)}) %collective-permute-start.12) | collective-permute-done | bytes 196640 | tf_op jit(solution)/shard_map/ppermute | solution.py:301
  85.9 1.4 %collective-permute-done.11.refs_2_ = bf16[3,64,512]{2,1,0:T(8,128)(2,1)S(1)} collective-permute-done((bf16[3,64,512]{2,1,0:T(8,128)(2,1)S(1)}, bf16[3,64,512]{2,1,0:T(8,128)(2,1)S(1)}, u32[]{:S(2)}, u32[]{:S(2)}) %collective-permute-start.11) | collective-permute-done | bytes 196640 | tf_op jit(solution)/shard_map/ppermute | solution.py:301
  89.9 2.1 %shard_map.154 = f32[320,512]{1,0:T(8,128)} custom-call(s32[32,12]{1,0:T(8,128)S(1)} %reshape.26.rows_ref, bf16[384,512]{1,0:T(8,128)(2,1)S(1)} %copy-done.6, bf16[512,512]{1,0:T(8,128)(2,1)S(1)} %copy-done.9, f32[3,64,512]{2,1,0:T(8,128)S(1)} %get-tuple-element.33.refs_0_.after_ref), custom_call_target="tpu_custom_call" | custom-call | flops 671088640 | tf_op jit(solution)/shard_map/pallas_call | solution.py:52
  92.0 5.1 %shard_map.153 = (f32[4096,512]{1,0:T(8,128)}, f32[1,512]{1,0:T(1,128)}) custom-call(s32[32,12]{1,0:T(8,128)S(1)} %bitcast.6, bf16[32,8,896]{2,1,0:T(8,128)(2,1)S(1)} %all-to-all-done.2.came_ref, bf16[3,64,512]{2,1,0:T(8,128)(2,1)S(1)} %shard_map.152.after_ref.refs_0_), custom_call_target="tpu_custom_call" | custom-call | flops 1610612736 | bytes 8388608 | tf_op jit(solution)/shard_map/pallas_call | solution.py:423
  97.1 1.8 %shard_map.155 = (f32[512,512]{1,0:T(8,128)}, f32[512,512]{1,0:T(8,128)}, f32[512,512]{1,0:T(8,128)}) custom-call(bf16[3,64,512]{2,1,0:T(8,128)(2,1)S(1)} %shard_map.152.after_ref.refs_0_, bf16[3,64,512]{2,1,0:T(8,128)(2,1)S(1)} %collective-permute-done.10.refs_1_, bf16[3,64,512]{2,1,0:T(8,128)(2,1)S(1)} %collective-permute-done.11.refs_2_, ...), custom_call_target="tpu_custom_call" | custom-call | tf_op jit(solution)/shard_map/pallas_call | solution.py:442
  (59 shorter events, 13.1 us)
Async XLA Ops:
  0.6 22.2 %copy-start.14 = (s32[1,32]{1,0:T(1,128)S(1)}, s32[1,32]{1,0:T(1,128)}, u32[]{:S(2)}) copy-start(s32[1,32]{1,0:T(1,128)} %param.15) | copy-start | bytes 388
  0.7 22.2 %copy-start.8 = (bf16[512,512]{1,0:T(8,128)(2,1)S(1)}, bf16[512,512]{1,0:T(8,128)(2,1)}, u32[]{:S(2)}) copy-start(bf16[512,512]{1,0:T(8,128)(2,1)} %w1_ref.7) | copy-start | bytes 1572868
  0.7 22.2 %copy-start.7 = (bf16[512,512]{1,0:T(8,128)(2,1)S(1)}, bf16[512,512]{1,0:T(8,128)(2,1)}, u32[]{:S(2)}) copy-start(bf16[512,512]{1,0:T(8,128)(2,1)} %w2_ref.1) | copy-start | bytes 1572868
  0.7 22.2 %copy-start.12 = (f32[512]{0:T(512)S(1)}, f32[512]{0:T(512)}, u32[]{:S(2)}) copy-start(f32[512]{0:T(512)} %param.18) | copy-start | bytes 6148
  0.7 22.2 %copy-start.10 = (bf16[320,512]{1,0:T(8,128)(2,1)S(1)}, bf16[320,512]{1,0:T(8,128)(2,1)}, u32[]{:S(2)}) copy-start(bf16[320,512]{1,0:T(8,128)(2,1)} %latent_ref.1) | copy-start | bytes 983044
  20.1 15.9 %all-to-all-start.1 = ((bf16[32,8,768]{2,1,0:T(8,128)(2,1)}), bf16[32,8,768]{2,1,0:T(8,128)(2,1)S(1)}, u32[]{:S(2)}, u32[]{:S(2)}) async-start(bf16[32,8,768]{2,1,0:T(8,128)(2,1)} %shard_map.145), calls=%async_computation.1 | async-start | bytes 786432 | tf_op jit(solution)/shard_map/all_to_all | solution.py:377
  40.3 4.6 %collective-permute-start = (bf16[3,256,512]{2,1,0:T(8,128)(2,1)}, bf16[3,256,512]{2,1,0:T(8,128)(2,1)S(1)}, u32[]{:S(2)}, u32[]{:S(2)}) collective-permute-start(bf16[3,256,512]{2,1,0:T(8,128)(2,1)} %get-tuple-element.32), channel_id=1, source_target_pairs={{0,1},{1,0},{2,3},{3,2},{4,5},{5,4},{6,7},{7,6},{8,9},{9,8},{10,11... | collective-permute-start | bytes 2359304 | tf_op jit(solution)/shard_map/ppermute | solution.py:301
  42.3 49.7 %all-to-all-start.2 = ((bf16[32,8,896]{2,1,0:T(8,128)(2,1)}), bf16[32,8,896]{2,1,0:T(8,128)(2,1)S(1)}, u32[]{:S(2)}, u32[]{:S(2)}) async-start(bf16[32,8,896]{2,1,0:T(8,128)(2,1)} %shard_map.148), calls=%async_computation.2 | async-start | bytes 917504 | tf_op jit(solution)/shard_map/all_to_all | solution.py:409
  45.1 11.9 %collective-permute-start.1 = (bf16[3,64,512]{2,1,0:T(8,128)(2,1)S(1)}, bf16[3,64,512]{2,1,0:T(8,128)(2,1)S(1)}, u32[]{:S(2)}, u32[]{:S(2)}) collective-permute-start(bf16[3,64,512]{2,1,0:T(8,128)(2,1)S(1)} %get-tuple-element.34), channel_id=1, source_target_pairs={{0,2},{1,3},{2,0},{3,1},{4,6},{5,7},{6,4},{7,5},{8,10},{9,11},{10,... | collective-permute-start | bytes 589832 | tf_op jit(solution)/shard_map/ppermute | solution.py:301
  46.9 10.2 %collective-permute-start.2 = (bf16[3,64,512]{2,1,0:T(8,128)(2,1)S(1)}, bf16[3,64,512]{2,1,0:T(8,128)(2,1)S(1)}, u32[]{:S(2)}, u32[]{:S(2)}) collective-permute-start(bf16[3,64,512]{2,1,0:T(8,128)(2,1)S(1)} %get-tuple-element.35), channel_id=1, source_target_pairs={{0,4},{1,5},{2,6},{3,7},{4,0},{5,1},{6,2},{7,3},{8,12},{9,13},{10,... | collective-permute-start | bytes 589832 | tf_op jit(solution)/shard_map/ppermute | solution.py:301
  48.3 13.6 %collective-permute-start.3 = (bf16[3,64,512]{2,1,0:T(8,128)(2,1)S(1)}, bf16[3,64,512]{2,1,0:T(8,128)(2,1)S(1)}, u32[]{:S(2)}, u32[]{:S(2)}) collective-permute-start(bf16[3,64,512]{2,1,0:T(8,128)(2,1)S(1)} %get-tuple-element.36), channel_id=1, source_target_pairs={{0,6},{1,7},{2,4},{3,5},{4,2},{5,3},{6,0},{7,1},{8,14},{9,15},{10,... | collective-permute-start | bytes 589832 | tf_op jit(solution)/shard_map/ppermute | solution.py:301
  62.0 4.5 %collective-permute-start.4 = (bf16[3,16,512]{2,1,0:T(8,128)(2,1)S(1)}, bf16[3,16,512]{2,1,0:T(8,128)(2,1)S(1)}, u32[]{:S(2)}, u32[]{:S(2)}) collective-permute-start(bf16[3,16,512]{2,1,0:T(8,128)(2,1)S(1)} %get-tuple-element.38), channel_id=1, source_target_pairs={{0,8},{1,9},{2,10},{3,11},{4,12},{5,13},{6,14},{7,15},{8,0},{9,1},... | collective-permute-start | bytes 147464 | tf_op jit(solution)/shard_map/ppermute | solution.py:301
  63.6 5.6 %collective-permute-start.5 = (bf16[3,16,512]{2,1,0:T(8,128)(2,1)S(1)}, bf16[3,16,512]{2,1,0:T(8,128)(2,1)S(1)}, u32[]{:S(2)}, u32[]{:S(2)}) collective-permute-start(bf16[3,16,512]{2,1,0:T(8,128)(2,1)S(1)} %get-tuple-element.39), channel_id=1, source_target_pairs={{0,16},{1,17},{2,18},{3,19},{4,20},{5,21},{6,22},{7,23},{8,24},{9,... | collective-permute-start | bytes 147464 | tf_op jit(solution)/shard_map/ppermute | solution.py:301
  66.0 5.9 %collective-permute-start.6 = (bf16[3,16,512]{2,1,0:T(8,128)(2,1)S(1)}, bf16[3,16,512]{2,1,0:T(8,128)(2,1)S(1)}, u32[]{:S(2)}, u32[]{:S(2)}) collective-permute-start(bf16[3,16,512]{2,1,0:T(8,128)(2,1)S(1)} %get-tuple-element.40), channel_id=1, source_target_pairs={{0,24},{1,25},{2,26},{3,27},{4,28},{5,29},{6,30},{7,31},{8,16},{9,... | collective-permute-start | bytes 147464 | tf_op jit(solution)/shard_map/ppermute | solution.py:301
  72.0 6.1 %collective-permute-start.9 = (bf16[3,16,512]{2,1,0:T(8,128)(2,1)S(1)}, bf16[3,16,512]{2,1,0:T(8,128)(2,1)S(1)}, u32[]{:S(2)}, u32[]{:S(2)}) collective-permute-start(bf16[3,16,512]{2,1,0:T(8,128)(2,1)S(1)} %shard_map.151.refs_0_), channel_id=1, source_target_pairs={{0,24},{1,25},{2,26},{3,27},{4,28},{5,29},{6,30},{7,31},{8,16},{9,... | collective-permute-start | bytes 147464 | tf_op jit(solution)/shard_map/ppermute | solution.py:301
  72.6 6.0 %collective-permute-start.8 = (bf16[3,16,512]{2,1,0:T(8,128)(2,1)S(1)}, bf16[3,16,512]{2,1,0:T(8,128)(2,1)S(1)}, u32[]{:S(2)}, u32[]{:S(2)}) collective-permute-start(bf16[3,16,512]{2,1,0:T(8,128)(2,1)S(1)} %shard_map.151.refs_0_), channel_id=1, source_target_pairs={{0,16},{1,17},{2,18},{3,19},{4,20},{5,21},{6,22},{7,23},{8,24},{9,... | collective-permute-start | bytes 147464 | tf_op jit(solution)/shard_map/ppermute | solution.py:301
  72.7 6.0 %collective-permute-start.7 = (bf16[3,16,512]{2,1,0:T(8,128)(2,1)S(1)}, bf16[3,16,512]{2,1,0:T(8,128)(2,1)S(1)}, u32[]{:S(2)}, u32[]{:S(2)}) collective-permute-start(bf16[3,16,512]{2,1,0:T(8,128)(2,1)S(1)} %shard_map.151.refs_0_), channel_id=1, source_target_pairs={{0,8},{1,9},{2,10},{3,11},{4,12},{5,13},{6,14},{7,15},{8,0},{9,1},... | collective-permute-start | bytes 147464 | tf_op jit(solution)/shard_map/ppermute | solution.py:301
  78.7 7.2 %collective-permute-start.12 = (bf16[3,64,512]{2,1,0:T(8,128)(2,1)S(1)}, bf16[3,64,512]{2,1,0:T(8,128)(2,1)S(1)}, u32[]{:S(2)}, u32[]{:S(2)}) collective-permute-start(bf16[3,64,512]{2,1,0:T(8,128)(2,1)S(1)} %shard_map.152.after_ref.refs_0_), channel_id=1, source_target_pairs={{0,6},{1,7},{2,4},{3,5},{4,2},{5,3},{6,0},{7,1},{8,14},{9,15},{10,... | collective-permute-start | bytes 589832 | tf_op jit(solution)/shard_map/ppermute | solution.py:301
  79.5 7.8 %collective-permute-start.11 = (bf16[3,64,512]{2,1,0:T(8,128)(2,1)S(1)}, bf16[3,64,512]{2,1,0:T(8,128)(2,1)S(1)}, u32[]{:S(2)}, u32[]{:S(2)}) collective-permute-start(bf16[3,64,512]{2,1,0:T(8,128)(2,1)S(1)} %shard_map.152.after_ref.refs_0_), channel_id=1, source_target_pairs={{0,4},{1,5},{2,6},{3,7},{4,0},{5,1},{6,2},{7,3},{8,12},{9,13},{10,... | collective-permute-start | bytes 589832 | tf_op jit(solution)/shard_map/ppermute | solution.py:301
  80.9 6.4 %collective-permute-start.10 = (bf16[3,64,512]{2,1,0:T(8,128)(2,1)S(1)}, bf16[3,64,512]{2,1,0:T(8,128)(2,1)S(1)}, u32[]{:S(2)}, u32[]{:S(2)}) collective-permute-start(bf16[3,64,512]{2,1,0:T(8,128)(2,1)S(1)} %shard_map.152.after_ref.refs_0_), channel_id=1, source_target_pairs={{0,2},{1,3},{2,0},{3,1},{4,6},{5,7},{6,4},{7,5},{8,10},{9,11},{10,... | collective-permute-start | bytes 589832 | tf_op jit(solution)/shard_map/ppermute | solution.py:301
  82.2 14.8 %collective-permute-start.13 = (bf16[3,64,512]{2,1,0:T(8,128)(2,1)S(1)}, bf16[3,64,512]{2,1,0:T(8,128)(2,1)S(1)}, u32[]{:S(2)}, u32[]{:S(2)}) collective-permute-start(bf16[3,64,512]{2,1,0:T(8,128)(2,1)S(1)} %shard_map.152.after_ref.refs_0_), channel_id=1, source_target_pairs={{0,1},{1,0},{2,3},{3,2},{4,5},{5,4},{6,7},{7,6},{8,9},{9,8},{10,11... | collective-permute-start | bytes 589832 | tf_op jit(solution)/shard_map/ppermute | solution.py:301
  85.9 11.2 %collective-permute-start.16 = (bf16[3,64,512]{2,1,0:T(8,128)(2,1)S(1)}, bf16[3,64,512]{2,1,0:T(8,128)(2,1)S(1)}, u32[]{:S(2)}, u32[]{:S(2)}) collective-permute-start(bf16[3,64,512]{2,1,0:T(8,128)(2,1)S(1)} %collective-permute-done.12.refs_3_), channel_id=1, source_target_pairs={{0,1},{1,0},{2,3},{3,2},{4,5},{5,4},{6,7},{7,6},{8,9},{9,8},{10,11... | collective-permute-start | bytes 589832 | tf_op jit(solution)/shard_map/ppermute | solution.py:301
  87.3 9.8 %collective-permute-start.15 = (bf16[3,64,512]{2,1,0:T(8,128)(2,1)S(1)}, bf16[3,64,512]{2,1,0:T(8,128)(2,1)S(1)}, u32[]{:S(2)}, u32[]{:S(2)}) collective-permute-start(bf16[3,64,512]{2,1,0:T(8,128)(2,1)S(1)} %collective-permute-done.11.refs_2_), channel_id=1, source_target_pairs={{0,1},{1,0},{2,3},{3,2},{4,5},{5,4},{6,7},{7,6},{8,9},{9,8},{10,11... | collective-permute-start | bytes 589832 | tf_op jit(solution)/shard_map/ppermute | solution.py:301
  87.3 9.8 %collective-permute-start.14 = (bf16[3,64,512]{2,1,0:T(8,128)(2,1)S(1)}, bf16[3,64,512]{2,1,0:T(8,128)(2,1)S(1)}, u32[]{:S(2)}, u32[]{:S(2)}) collective-permute-start(bf16[3,64,512]{2,1,0:T(8,128)(2,1)S(1)} %collective-permute-done.10.refs_1_), channel_id=1, source_target_pairs={{0,1},{1,0},{2,3},{3,2},{4,5},{5,4},{6,7},{7,6},{8,9},{9,8},{10,11... | collective-permute-start | bytes 589832 | tf_op jit(solution)/shard_map/ppermute | solution.py:301
  (10 other events, 49.1 us)
